TPU v7x, 128 devices: a whole 4x4x4 slice. The times are simulated.
128 devices in a mesh: tm: 2 (over core), space: 64 (over z, y, x).
Axes of the slice: x: 4, y: 4, z: 4, core: 2. Of those that a mesh axis runs over, the one named last changes fastest.
Arguments:
- fine: bfloat16 [8, 256, 256, 256], P('tm', 'space'), may hold values from -6 to 6
- coarse: bfloat16 [8, 128, 128, 256], P('tm', 'space'), may hold values from -6 to 6
- w_query: bfloat16 [256, 256], replicated, may hold values from -24 to 24
- w_key: bfloat16 [256, 256], replicated, may hold values from -0.375 to 0.375
- w_value: bfloat16 [256, 256], replicated, may hold values from -0.375 to 0.375
- w_out: bfloat16 [256, 256], replicated, may hold values from -0.375 to 0.375
- conv_first: bfloat16 [3, 3, 256, 256], replicated, may hold values from -0.125 to 0.125
- conv_second: bfloat16 [3, 3, 256, 256], replicated, may hold values from -0.125 to 0.125
Outputs:
- joined: bfloat16 [8, 256, 256, 256], P('tm', 'space')
All inputs are finite; a program needn't handle non-finite values.
Results may differ from a plain program's by a relative error of at most 0.009.
Values may be sent and summed in bfloat16 or wider, within the bound.
No kernel may reach another device: no remote copies, remote signals or barrier semaphores. Data moves between devices by JAX's collectives and lax.ppermute only.
A program may use at most 128 MiB of HBM per device.

v0:
```python
import jax
import jax.numpy as jnp
import numpy as np
from jax import lax
from jax.experimental import pallas as pl
from jax.experimental.pallas import tpu as pltpu
from jax.sharding import PartitionSpec as P

HEADS = 8
C = 256
D = C // HEADS
W = 256
F32 = jnp.float32
BF16 = jnp.bfloat16
VMEM_LIMIT = 56 * 1024 * 1024


def encode_table(frames, width):
    half = width // 2
    inverse = np.exp(-np.log(10000.0) * 2.0 * np.arange(half) / width)
    angles = np.arange(frames)[:, None] * inverse[None, :]
    table = np.concatenate([np.sin(angles), np.cos(angles)], axis=1)
    return table.astype(np.float32)


def dot(a, b):
    return jnp.dot(a, b, preferred_element_type=F32)


def attention_body(pos_ref, own_ref, other_ref, wq_ref, wk_ref, wv_ref, wo_ref,
                   moved_ref, up_ref, down_ref,
                   wqkv_s, wo_s, norm_s, q_s, k_s, v_s, att_s):
    row = pl.program_id(0)
    frames = own_ref.shape[0]

    @pl.when(row == 0)
    def _():
        to = lax.broadcasted_iota(jnp.int32, (C, C), 0)
        at = lax.broadcasted_iota(jnp.int32, (C, C), 1)
        pick = (at == (to % HEADS) * D + to // HEADS).astype(BF16)
        nt = (((1,), (1,)), ((), ()))
        for n, ref in enumerate((wq_ref, wk_ref, wv_ref)):
            wqkv_s[n * C:(n + 1) * C] = lax.dot_general(pick, ref[...], nt, preferred_element_type=F32).astype(BF16)
        wo_s[...] = dot(pick, wo_ref[...]).astype(BF16)

    for f in range(2 * frames):
        x_ref = own_ref if f < frames else other_ref
        i = f % frames
        for half in range(W // 128):
            lanes = slice(half * 128, half * 128 + 128)
            xt = x_ref[i, 0, lanes, :].T
            h = xt.astype(F32) + pos_ref[f]
            center = h - jnp.sum(h, axis=0, keepdims=True) * (1.0 / C)
            spread = jnp.sum(center * center, axis=0, keepdims=True) * (1.0 / C)
            norm_s[f % 2, :, lanes] = (center * lax.rsqrt(spread + 1e-05)).astype(BF16)
        if f < frames:
            y = dot(wqkv_s[...], norm_s[f % 2])
            q_s[i] = y[:C]
            k_s[f] = y[C:2 * C]
            v_s[f] = y[2 * C:]
        else:
            y = dot(wqkv_s[C:], norm_s[f % 2])
            k_s[f] = y[:C]
            v_s[f] = y[C:]

    factor = float(np.log2(np.e) / np.sqrt(D))
    keys = 2 * frames
    for half in range(W // 128):
        lanes = slice(half * 128, half * 128 + 128)

        def score(d, acc):
            at = pl.ds(pl.multiple_of(d * HEADS, HEADS), HEADS)
            qs = [q_s[a, at, lanes] for a in range(frames)]
            ks = [k_s[b, at, lanes] for b in range(keys)]
            return tuple(acc[a * keys + b] + qs[a] * ks[b] for a in range(frames) for b in range(keys))

        zero = jnp.zeros((HEADS, 128), F32)
        acc = lax.fori_loop(0, D, score, (zero,) * (frames * keys), unroll=4)
        weights = []
        for a in range(frames):
            line = acc[a * keys:(a + 1) * keys]
            top = line[0]
            for s in line[1:]:
                top = jnp.maximum(top, s)
            powers = [jnp.exp2((s - top) * factor) for s in line]
            total = powers[0]
            for p in powers[1:]:
                total = total + p
            inv = 1.0 / total
            weights += [p * inv for p in powers]

        def gather(d2, _):
            outs = [[] for _ in range(frames)]
            for sub in range(2):
                at = pl.ds(pl.multiple_of(d2 * 2 * HEADS + sub * HEADS, HEADS), HEADS)
                vs = [v_s[b, at, lanes] for b in range(keys)]
                for a in range(frames):
                    total = weights[a * keys] * vs[0]
                    for b in range(1, keys):
                        total = total + weights[a * keys + b] * vs[b]
                    outs[a].append(total)
            at = pl.ds(pl.multiple_of(d2 * 2 * HEADS, 2 * HEADS), 2 * HEADS)
            for a in range(frames):
                att_s[a, at, lanes] = jnp.concatenate(outs[a], axis=0).astype(BF16)
            return 0

        lax.fori_loop(0, D // 2, gather, 0, unroll=2)

    for a in range(frames):
        branch = lax.dot_general(att_s[a], wo_s[...], (((0,), (0,)), ((), ())), preferred_element_type=F32)
        moved = (own_ref[a, 0].astype(F32) + branch).astype(BF16)
        moved_ref[a, 0] = moved
        up_ref[a, 0] = moved

        @pl.when(row <= 1)
        def _():
            down_ref[a, 0] = moved


def attention(pos, own, other, w_query, w_key, w_value, w_out):
    frames, rows = own.shape[:2]
    block = (frames, 1, W, C)
    by_row = pl.BlockSpec(block, lambda r: (0, r, 0, 0))
    whole = pl.BlockSpec((C, C), lambda r: (0, 0))
    return pl.pallas_call(
        attention_body,
        grid=(rows,),
        in_specs=[pl.BlockSpec(pos.shape, lambda r: (0, 0, 0)), by_row, by_row, whole, whole, whole, whole],
        out_specs=[by_row,
                   pl.BlockSpec(block, lambda r: (0, jnp.maximum(r - (rows - 2), 0), 0, 0)),
                   pl.BlockSpec(block, lambda r: (0, jnp.minimum(r, 1), 0, 0))],
        out_shape=[jax.ShapeDtypeStruct(own.shape, BF16),
                   jax.ShapeDtypeStruct((frames, 2, W, C), BF16),
                   jax.ShapeDtypeStruct((frames, 2, W, C), BF16)],
        scratch_shapes=[pltpu.VMEM((3 * C, C), BF16), pltpu.VMEM((C, C), BF16),
                        pltpu.VMEM((2, C, W), BF16),
                        pltpu.VMEM((frames, C, W), F32), pltpu.VMEM((2 * frames, C, W), F32),
                        pltpu.VMEM((2 * frames, C, W), F32), pltpu.VMEM((frames, C, W), BF16)],
        compiler_params=pltpu.CompilerParams(dimension_semantics=("arbitrary",), vmem_limit_bytes=VMEM_LIMIT),
        name="attention",
    )(pos, own, other, w_query, w_key, w_value, w_out)


def shifted(value, pad_s, out, at):
    pad_s[8:8 + W] = value.astype(F32)
    out[1, at] = value
    out[0, at] = pad_s[7:7 + W].astype(BF16)
    out[2, at] = pad_s[9:9 + W].astype(BF16)


def conv_body(edge_ref, moved_ref, above_ref, below_ref, coarse_ref, ca_ref, cb_ref, w1_ref, w2_ref,
              out_ref, pad_s, in_s, mid_s, coarse_s, lift_s):
    rows = moved_ref.shape[1]
    first_edge = edge_ref[0] == 1
    last_edge = edge_ref[1] == 1

    @pl.when(pl.program_id(0) == 0)
    def _():
        pad_s[0:8] = jnp.zeros((8, C), F32)
        pad_s[8 + W:16 + W] = jnp.zeros((8, C), F32)
        x = lax.broadcasted_iota(jnp.int32, (W, W), 0)
        at = lax.broadcasted_iota(jnp.int32, (W, W), 1)
        high = at // (W // 2)
        col = at % (W // 2)
        near = x // 2
        far = jnp.clip(near + 2 * (x % 2) - 1, 0, W // 2 - 1)
        base = 0.75 * (col == near).astype(F32) + 0.25 * (col == far).astype(F32)
        lift_s[0] = (base * jnp.where(high == 1, 0.75, 0.25)).astype(BF16)
        lift_s[1] = (base * jnp.where(high == 1, 0.25, 0.75)).astype(BF16)

    half = W // 2
    coarse_rows = rows // 2
    top = coarse_ref[0, 0]
    bottom = coarse_ref[0, coarse_rows - 1]
    coarse_s[0:half] = jnp.where(first_edge, top, ca_ref[0, 0])
    for r in range(coarse_rows):
        coarse_s[half * (r + 1):half * (r + 2)] = coarse_ref[0, r]
    coarse_s[half * (coarse_rows + 1):half * (coarse_rows + 2)] = jnp.where(last_edge, bottom, cb_ref[0, 0])

    zero = jnp.zeros((), BF16)
    for r in range(rows + 4):
        if r < 2:
            value = above_ref[0, r]
        elif r < rows + 2:
            value = moved_ref[0, r - 2]
        else:
            value = below_ref[0, r - rows - 2]
        shifted(jnp.maximum(value, zero), pad_s, in_s, slice(r * W, (r + 1) * W))

    def first(j, _):
        start = pl.multiple_of(j * W, W)
        total = None
        for dy in range(3):
            for dx in range(3):
                part = dot(in_s[dx, pl.ds(start + dy * W, W)], w1_ref[dy, dx])
                total = part if total is None else total + part
        value = jnp.maximum(total, 0.0).astype(BF16)
        outside = jnp.logical_or(jnp.logical_and(first_edge, j == 0), jnp.logical_and(last_edge, j == rows + 1))
        value = jnp.where(outside, jnp.zeros_like(value), value)
        shifted(value, pad_s, mid_s, pl.ds(start, W))
        return 0

    lax.fori_loop(0, rows + 2, first, 0)

    for j in range(rows):
        total = dot(lift_s[j % 2], coarse_s[((j + 1) // 2) * half:((j + 1) // 2) * half + W])
        for dy in range(3):
            for dx in range(3):
                total = total + dot(mid_s[dx, (j + dy) * W:(j + dy + 1) * W], w2_ref[dy, dx])
        out_ref[0, j] = (total + moved_ref[0, j].astype(F32)).astype(BF16)


def convolutions(edge, moved, above, below, coarse, ca, cb, conv_first, conv_second):
    frames, rows = moved.shape[:2]
    coarse_rows = coarse.shape[1]

    def by_frame(n, w):
        return pl.BlockSpec((1, n, w, C), lambda f: (f, 0, 0, 0))

    whole = pl.BlockSpec(conv_first.shape, lambda f: (0, 0, 0, 0))
    return pl.pallas_call(
        conv_body,
        grid=(frames,),
        in_specs=[pl.BlockSpec(memory_space=pltpu.SMEM), by_frame(rows, W), by_frame(2, W), by_frame(2, W),
                  by_frame(coarse_rows, W // 2), by_frame(1, W // 2), by_frame(1, W // 2), whole, whole],
        out_specs=by_frame(rows, W),
        out_shape=jax.ShapeDtypeStruct(moved.shape, BF16),
        scratch_shapes=[pltpu.VMEM((W + 16, C), F32), pltpu.VMEM((3, (rows + 4) * W, C), BF16),
                        pltpu.VMEM((3, (rows + 2) * W, C), BF16),
                        pltpu.VMEM(((coarse_rows + 2) * W // 2, C), BF16), pltpu.VMEM((2, W, W), BF16)],
        compiler_params=pltpu.CompilerParams(dimension_semantics=("arbitrary",), vmem_limit_bytes=VMEM_LIMIT),
        name="convolutions",
    )(edge, moved, above, below, coarse, ca, cb, conv_first, conv_second)


def local(fine, coarse, w_query, w_key, w_value, w_out, conv_first, conv_second):
    frames = fine.shape[0]
    tm = lax.axis_index("tm")
    size = lax.axis_size("space")
    here = lax.axis_index("space")
    up = [(i, i + 1) for i in range(size - 1)]
    down = [(i + 1, i) for i in range(size - 1)]
    other = lax.ppermute(fine, "tm", [(0, 1), (1, 0)])
    ca = lax.ppermute(coarse[:, -1:], "space", up)
    cb = lax.ppermute(coarse[:, :1], "space", down)
    table = jnp.broadcast_to(jnp.asarray(encode_table(2 * frames, C))[:, :, None], (2 * frames, C, 128))
    pos = jnp.where(tm == 0, table, jnp.roll(table, frames, axis=0))
    moved, up_rows, down_rows = attention(pos, fine, other, w_query, w_key, w_value, w_out)
    above = lax.ppermute(up_rows, "space", up)
    below = lax.ppermute(down_rows, "space", down)
    edge = jnp.stack([here == 0, here == size - 1]).astype(jnp.int32)
    return convolutions(edge, moved, above, below, coarse, ca, cb, conv_first, conv_second)


def solution(mesh):
    split = P("tm", "space", None, None)
    return jax.shard_map(
        local,
        mesh=mesh,
        in_specs=(split, split, P(), P(), P(), P(), P(), P()),
        out_specs=split,
        check_vma=False,
    )
```

profile of v0, /device:TPU:30, one launch (start us, length us, event | category | flops | bytes accessed | tf_op | source)
XLA Modules:
  0.0 89.8 jit_solution(6049086306645728134)
XLA Ops:
  0.0 0.0 collective-permute-start
  0.0 0.9 broadcast_in_dim.11
  0.9 0.9 broadcast_in_dim.12
  1.8 2.0 %maximum_select_fusion.pos_ref = f32[8,256,128]{2,1,0:T(8,128)} fusion(f32[4,256,128]{2,1,0:T(8,128)S(1)} %broadcast_in_dim.12, f32[4,256,128]{2,1,0:T(8,128)S(1)} %broadcast_in_dim.11, f32[8,256]{1,0:T(8,128)} %constant.15.clone, pred[]{:T(512)S(6)} %eq.11), kind=kLoop, calls=%fused_computation | loop fusion | flops 524288 | bytes 2105345 | tf_op jit(solution)/shard_map/jit(_where)/select_n | solution.py:247
  3.8 0.0 copy-start
  3.8 0.6 collective-permute-done.other_ref
  4.4 0.0 copy-start.1
  4.4 1.3 %copy-done.1 = bf16[4,4,256,256]{3,2,1,0:T(8,128)(2,1)} copy-done((bf16[4,4,256,256]{3,2,1,0:T(8,128)(2,1)}, bf16[4,4,256,256]{3,2,1,0:T(8,128)(2,1)S(1)}, u32[]{:S(2)}) %copy-start.1) | copy-done | bytes 2097176
  5.7 18.3 %attention.1 = (bf16[4,4,256,256]{3,2,1,0:T(8,128)(2,1)}, bf16[4,2,256,256]{3,2,1,0:T(8,128)(2,1)}, bf16[4,2,256,256]{3,2,1,0:T(8,128)(2,1)}) custom-call(f32[8,256,128]{2,1,0:T(8,128)} %maximum_select_fusion.pos_ref, bf16[4,4,256,256]{3,2,1,0:T(8,128)(2,1)} %own_ref.1, bf16[4,4,256,256]{3,2,1,0:T(8,128)(2,1)} %copy-done.1, bf16[256,256]{1,0:T(8,128)(2,1)} %wq_ref.1, ...), custom_call_target="tpu_custom_call" | custom-call | tf_op jit(solution)/shard_map/attention/pallas_call | solution.py:125
  24.0 3.4 %collective-permute-start.1 = (bf16[4,2,256,256]{3,2,1,0:T(8,128)(2,1)}, bf16[4,2,256,256]{3,2,1,0:T(8,128)(2,1)S(1)}, u32[]{:S(2)}, u32[]{:S(2)}) collective-permute-start(bf16[4,2,256,256]{3,2,1,0:T(8,128)(2,1)} %get-tuple-element.9), channel_id=1, source_target_pairs={{0,1},{1,2},{2,3},{3,4},{4,5},{5,6},{6,7},{7,8},{8,9},{9,10},{10,1... | collective-permute-start | bytes 3145736 | tf_op jit(solution)/shard_map/ppermute | solution.py:249
  27.4 2.4 %collective-permute-start.2 = (bf16[4,2,256,256]{3,2,1,0:T(8,128)(2,1)}, bf16[4,2,256,256]{3,2,1,0:T(8,128)(2,1)S(1)}, u32[]{:S(2)}, u32[]{:S(2)}) collective-permute-start(bf16[4,2,256,256]{3,2,1,0:T(8,128)(2,1)} %get-tuple-element.10), channel_id=1, source_target_pairs={{1,0},{2,1},{3,2},{4,3},{5,4},{6,5},{7,6},{8,7},{9,8},{10,9},{11,1... | collective-permute-start | bytes 3145736 | tf_op jit(solution)/shard_map/ppermute | solution.py:250
  29.9 0.0 copy-done
  29.9 7.6 %collective-permute-start.3 = (bf16[4,1,128,256]{3,2,1,0:T(8,128)(2,1)S(1)}, bf16[4,1,128,256]{3,2,1,0:T(8,128)(2,1)S(1)}, u32[]{:S(2)}, u32[]{:S(2)}) collective-permute-start(bf16[4,1,128,256]{3,2,1,0:T(8,128)(2,1)S(1)} %get-tuple-element.12), channel_id=1, source_target_pairs={{0,1},{1,2},{2,3},{3,4},{4,5},{5,6},{6,7},{7,8},{8,9},{9,10},{10,1... | collective-permute-start | bytes 786440 | tf_op jit(solution)/shard_map/ppermute | solution.py:244
  37.5 1.9 %collective-permute-start.4 = (bf16[4,1,128,256]{3,2,1,0:T(8,128)(2,1)S(1)}, bf16[4,1,128,256]{3,2,1,0:T(8,128)(2,1)S(1)}, u32[]{:S(2)}, u32[]{:S(2)}) collective-permute-start(bf16[4,1,128,256]{3,2,1,0:T(8,128)(2,1)S(1)} %get-tuple-element.11), channel_id=1, source_target_pairs={{1,0},{2,1},{3,2},{4,3},{5,4},{6,5},{7,6},{8,7},{9,8},{10,9},{11,1... | collective-permute-start | bytes 786440 | tf_op jit(solution)/shard_map/ppermute | solution.py:245
  39.5 0.7 add_convert_fusion.edge_ref
  40.1 16.8 %collective-permute-done.3.ca_ref = bf16[4,1,128,256]{3,2,1,0:T(8,128)(2,1)S(1)} collective-permute-done((bf16[4,1,128,256]{3,2,1,0:T(8,128)(2,1)S(1)}, bf16[4,1,128,256]{3,2,1,0:T(8,128)(2,1)S(1)}, u32[]{:S(2)}, u32[]{:S(2)}) %collective-permute-start.3) | collective-permute-done | bytes 262176 | tf_op jit(solution)/shard_map/ppermute | solution.py:244
  56.9 0.0 copy-start.4
  56.9 7.3 %collective-permute-done.4.cb_ref = bf16[4,1,128,256]{3,2,1,0:T(8,128)(2,1)S(1)} collective-permute-done((bf16[4,1,128,256]{3,2,1,0:T(8,128)(2,1)S(1)}, bf16[4,1,128,256]{3,2,1,0:T(8,128)(2,1)S(1)}, u32[]{:S(2)}, u32[]{:S(2)}) %collective-permute-start.4) | collective-permute-done | bytes 262176 | tf_op jit(solution)/shard_map/ppermute | solution.py:245
  64.3 0.0 copy-start.5
  64.3 0.0 collective-permute-done.1.above_ref
  64.3 0.0 copy-start.2
  64.3 0.0 collective-permute-done.2.below_ref
  64.3 0.0 copy-start.3
  64.3 0.0 copy-done.4
  64.3 0.7 copy-done.5
  65.0 0.4 copy-done.2
  65.3 0.3 copy-done.3
  65.7 24.1 %convolutions.1 = bf16[4,4,256,256]{3,2,1,0:T(8,128)(2,1)} custom-call(s32[2]{0:T(128)} %add_convert_fusion.edge_ref, bf16[4,4,256,256]{3,2,1,0:T(8,128)(2,1)} %get-tuple-element.8.moved_ref, bf16[4,2,256,256]{3,2,1,0:T(8,128)(2,1)} %copy-done.2, bf16[4,2,256,256]{3,2,1,0:T(8,128)(2,1)} %copy-done.3, bf16[4,2,128,256]{3,2,1,0:T(8,128)(2,1)} %coarse_ref.1, ...), custom_call_target="tpu_custom_call" | custom-call | tf_op jit(solution)/shard_map/convolutions/pallas_call | solution.py:221
  (1 shorter events, 0.0 us)
Async XLA Ops:
  0.0 4.4 %collective-permute-start = (bf16[4,4,256,256]{3,2,1,0:T(8,128)(2,1)}, bf16[4,4,256,256]{3,2,1,0:T(8,128)(2,1)S(1)}, u32[]{:S(2)}, u32[]{:S(2)}) collective-permute-start(bf16[4,4,256,256]{3,2,1,0:T(8,128)(2,1)} %own_ref.1), channel_id=1, source_target_pairs={{0,64},{64,0},{1,65},{65,1},{2,66},{66,2},{3,67},{67,3},{4,68},{68... | collective-permute-start | bytes 6291464 | tf_op jit(solution)/shard_map/ppermute | solution.py:243
  3.8 26.1 %copy-start = (bf16[4,2,128,256]{3,2,1,0:T(8,128)(2,1)S(1)}, bf16[4,2,128,256]{3,2,1,0:T(8,128)(2,1)}, u32[]{:S(2)}) copy-start(bf16[4,2,128,256]{3,2,1,0:T(8,128)(2,1)} %coarse_ref.1) | copy-start | bytes 1572868
  4.4 1.3 %copy-start.1 = (bf16[4,4,256,256]{3,2,1,0:T(8,128)(2,1)}, bf16[4,4,256,256]{3,2,1,0:T(8,128)(2,1)S(1)}, u32[]{:S(2)}) copy-start(bf16[4,4,256,256]{3,2,1,0:T(8,128)(2,1)S(1)} %collective-permute-done.other_ref) | copy-start | bytes 6291460
  24.0 40.3 %collective-permute-start.1 = (bf16[4,2,256,256]{3,2,1,0:T(8,128)(2,1)}, bf16[4,2,256,256]{3,2,1,0:T(8,128)(2,1)S(1)}, u32[]{:S(2)}, u32[]{:S(2)}) collective-permute-start(bf16[4,2,256,256]{3,2,1,0:T(8,128)(2,1)} %get-tuple-element.9), channel_id=1, source_target_pairs={{0,1},{1,2},{2,3},{3,4},{4,5},{5,6},{6,7},{7,8},{8,9},{9,10},{10,1... | collective-permute-start | bytes 3145736 | tf_op jit(solution)/shard_map/ppermute | solution.py:249
  27.4 36.9 %collective-permute-start.2 = (bf16[4,2,256,256]{3,2,1,0:T(8,128)(2,1)}, bf16[4,2,256,256]{3,2,1,0:T(8,128)(2,1)S(1)}, u32[]{:S(2)}, u32[]{:S(2)}) collective-permute-start(bf16[4,2,256,256]{3,2,1,0:T(8,128)(2,1)} %get-tuple-element.10), channel_id=1, source_target_pairs={{1,0},{2,1},{3,2},{4,3},{5,4},{6,5},{7,6},{8,7},{9,8},{10,9},{11,1... | collective-permute-start | bytes 3145736 | tf_op jit(solution)/shard_map/ppermute | solution.py:250
  29.9 27.0 %collective-permute-start.3 = (bf16[4,1,128,256]{3,2,1,0:T(8,128)(2,1)S(1)}, bf16[4,1,128,256]{3,2,1,0:T(8,128)(2,1)S(1)}, u32[]{:S(2)}, u32[]{:S(2)}) collective-permute-start(bf16[4,1,128,256]{3,2,1,0:T(8,128)(2,1)S(1)} %get-tuple-element.12), channel_id=1, source_target_pairs={{0,1},{1,2},{2,3},{3,4},{4,5},{5,6},{6,7},{7,8},{8,9},{9,10},{10,1... | collective-permute-start | bytes 786440 | tf_op jit(solution)/shard_map/ppermute | solution.py:244
  37.5 26.7 %collective-permute-start.4 = (bf16[4,1,128,256]{3,2,1,0:T(8,128)(2,1)S(1)}, bf16[4,1,128,256]{3,2,1,0:T(8,128)(2,1)S(1)}, u32[]{:S(2)}, u32[]{:S(2)}) collective-permute-start(bf16[4,1,128,256]{3,2,1,0:T(8,128)(2,1)S(1)} %get-tuple-element.11), channel_id=1, source_target_pairs={{1,0},{2,1},{3,2},{4,3},{5,4},{6,5},{7,6},{8,7},{9,8},{10,9},{11,1... | collective-permute-start | bytes 786440 | tf_op jit(solution)/shard_map/ppermute | solution.py:245
  56.9 7.4 %copy-start.4 = (bf16[4,1,128,256]{3,2,1,0:T(8,128)(2,1)}, bf16[4,1,128,256]{3,2,1,0:T(8,128)(2,1)S(1)}, u32[]{:S(2)}) copy-start(bf16[4,1,128,256]{3,2,1,0:T(8,128)(2,1)S(1)} %collective-permute-done.3.ca_ref) | copy-start | bytes 786436
  64.3 0.7 copy-start.5
  64.3 1.1 %copy-start.2 = (bf16[4,2,256,256]{3,2,1,0:T(8,128)(2,1)}, bf16[4,2,256,256]{3,2,1,0:T(8,128)(2,1)S(1)}, u32[]{:S(2)}) copy-start(bf16[4,2,256,256]{3,2,1,0:T(8,128)(2,1)S(1)} %collective-permute-done.1.above_ref) | copy-start | bytes 3145732
  64.3 1.4 %copy-start.3 = (bf16[4,2,256,256]{3,2,1,0:T(8,128)(2,1)}, bf16[4,2,256,256]{3,2,1,0:T(8,128)(2,1)S(1)}, u32[]{:S(2)}) copy-start(bf16[4,2,256,256]{3,2,1,0:T(8,128)(2,1)S(1)} %collective-permute-done.2.below_ref) | copy-start | bytes 3145732
where the time goes:
time: 90.1 us; the launch traced here: 89.8 us
  Pallas kernels  42.4 us (47%)
  waiting for transfers between devices  24.7 us (27%)
  starting transfers between devices  15.4 us (17%)
  local copies, waits for them, and re-layouts  4.5 us (5%)
  other arithmetic  2.67 us (3%)
    pallas_call x1, Pallas kernels, convolutions(): pl.pallas_call(conv_body, grid=(frames,), in_specs=[pl.BlockSpec(memory_s...  24.1 us
    pallas_call x1, Pallas kernels, attention(): pl.pallas_call(attention_body, grid=(rows,), in_specs=[pl.BlockSpec(pos.s...  18.3 us
    ppermute x1, waiting for transfers between devices, local(): ca = lax.ppermute(coarse[:, -1:], 'space', up)  16.8 us
    ppermute x1, starting transfers between devices, local(): ca = lax.ppermute(coarse[:, -1:], 'space', up)  7.62 us
    ppermute x1, waiting for transfers between devices, local(): cb = lax.ppermute(coarse[:, :1], 'space', down)  7.34 us
    ppermute x1, starting transfers between devices, local(): above = lax.ppermute(up_rows, 'space', up)  3.39 us
    unnamed x12, local copies, waits for them, and re-layouts  2.71 us
    ppermute x1, starting transfers between devices, local(): below = lax.ppermute(down_rows, 'space', down)  2.44 us
  transfers between devices with their start and end apart: 5, of which 3 were waited for; matrix products, arithmetic and copies ran while one was open for 5% of the time, Pallas kernels for 0%

commit v1 on v0

v1 whole, which is shorter than its diff:
```python
import jax
import jax.numpy as jnp
import numpy as np
from jax import lax
from jax.experimental import pallas as pl
from jax.experimental.pallas import tpu as pltpu
from jax.sharding import PartitionSpec as P

HEADS = 8
C = 256
D = C // HEADS
W = 256
HALF = W // 2
F32 = jnp.float32
BF16 = jnp.bfloat16
VMEM_LIMIT = 20 * 1024 * 1024


def encode_table(frames, width):
    half = width // 2
    inverse = np.exp(-np.log(10000.0) * 2.0 * np.arange(half) / width)
    angles = np.arange(frames)[:, None] * inverse[None, :]
    table = np.concatenate([np.sin(angles), np.cos(angles)], axis=1).astype(np.float32)
    return np.ascontiguousarray(np.broadcast_to(table[:, :, None], (frames, width, 128)))


def dot(a, b):
    return jnp.dot(a, b, preferred_element_type=F32)


def normed_row(x_ref, i, row, pos, norm):
    for half in range(W // 128):
        lanes = slice(half * 128, half * 128 + 128)
        h = x_ref[i, row, lanes, :].T.astype(F32) + pos
        center = h - jnp.sum(h, axis=0, keepdims=True) * (1.0 / C)
        spread = jnp.sum(center * center, axis=0, keepdims=True) * (1.0 / C)
        norm[:, lanes] = (center * lax.rsqrt(spread + 1e-05)).astype(BF16)


def attention_row(row, pos_ref, own_ref, other_ref, wkv_ref, wo_ref, q_ref, ko_ref, vo_ref, out_ref,
                  norm_s, k_s, v_s, att_s):
    frames = own_ref.shape[0]
    keys = 2 * frames
    base = (1 - lax.axis_index("tm")) * frames

    for f in range(frames):
        normed_row(other_ref, f, row, pos_ref[base + f], norm_s.at[f])
        y = dot(wkv_ref[C:], norm_s[f])
        k_s[f] = y[:C]
        v_s[f] = y[C:]

    factor = float(np.log2(np.e) / np.sqrt(D))
    for half in range(W // 128):
        lanes = slice(half * 128, half * 128 + 128)

        def score(d, acc):
            at = pl.ds(pl.multiple_of(d * HEADS, HEADS), HEADS)
            qs = [q_ref[row, a, at, lanes] for a in range(frames)]
            ks = [ko_ref[row, b, at, lanes] for b in range(frames)] + [k_s[b, at, lanes] for b in range(frames)]
            return tuple(acc[a * keys + b] + qs[a] * ks[b] for a in range(frames) for b in range(keys))

        zero = jnp.zeros((HEADS, 128), F32)
        acc = lax.fori_loop(0, D, score, (zero,) * (frames * keys), unroll=4)
        weights = []
        for a in range(frames):
            line = acc[a * keys:(a + 1) * keys]
            top = line[0]
            for s in line[1:]:
                top = jnp.maximum(top, s)
            powers = [jnp.exp2((s - top) * factor) for s in line]
            total = powers[0]
            for p in powers[1:]:
                total = total + p
            inv = 1.0 / total
            weights += [p * inv for p in powers]

        def gather(d2, _):
            outs = [[] for _ in range(frames)]
            for sub in range(2):
                at = pl.ds(pl.multiple_of(d2 * 2 * HEADS + sub * HEADS, HEADS), HEADS)
                vs = [vo_ref[row, b, at, lanes] for b in range(frames)] + [v_s[b, at, lanes] for b in range(frames)]
                for a in range(frames):
                    total = weights[a * keys] * vs[0]
                    for b in range(1, keys):
                        total = total + weights[a * keys + b] * vs[b]
                    outs[a].append(total)
            at = pl.ds(pl.multiple_of(d2 * 2 * HEADS, 2 * HEADS), 2 * HEADS)
            for a in range(frames):
                att_s[a, at, lanes] = jnp.concatenate(outs[a], axis=0).astype(BF16)
            return 0

        lax.fori_loop(0, D // 2, gather, 0, unroll=2)

    for a in range(frames):
        branch = lax.dot_general(att_s[a], wo_ref[...], (((0,), (0,)), ((), ())), preferred_element_type=F32)
        out_ref[a, :W] = (own_ref[a, row].astype(F32) + branch).astype(BF16)


def own_body(pos_hbm, own_hbm, wq_hbm, wk_hbm, wv_hbm, wo_hbm,
             pos_ref, own_ref, wqkv_ref, wor_ref, q_ref, k_ref, v_ref, w_s, norm_s, sems):
    frames, rows = own_hbm.shape[:2]
    loads = [pltpu.make_async_copy(ref, w_s.at[n], sems.at[n]) for n, ref in enumerate((wq_hbm, wk_hbm, wv_hbm, wo_hbm))]
    loads.append(pltpu.make_async_copy(pos_hbm, pos_ref, sems.at[4]))
    loads.append(pltpu.make_async_copy(own_hbm, own_ref, sems.at[5]))
    for load in loads:
        load.start()
    to = lax.broadcasted_iota(jnp.int32, (C, C), 0)
    at = lax.broadcasted_iota(jnp.int32, (C, C), 1)
    pick = (at == (to % HEADS) * D + to // HEADS).astype(BF16)
    nt = (((1,), (1,)), ((), ()))
    for load in loads[:4]:
        load.wait()
    for n in range(3):
        wqkv_ref[n * C:(n + 1) * C] = lax.dot_general(pick, w_s[n], nt, preferred_element_type=F32).astype(BF16)
    wor_ref[...] = dot(pick, w_s[3]).astype(BF16)
    for load in loads[4:]:
        load.wait()
    base = lax.axis_index("tm") * frames

    def one(row, _):
        for f in range(frames):
            normed_row(own_ref, f, row, pos_ref[base + f], norm_s.at[f])
            y = dot(wqkv_ref[...], norm_s[f])
            q_ref[row, f] = y[:C]
            k_ref[row, f] = y[C:2 * C]
            v_ref[row, f] = y[2 * C:]
        return 0

    lax.fori_loop(0, rows, one, 0)


def outer_body(pos_ref, own_ref, other_ref, wqkv_ref, wo_ref, q_ref, k_ref, v_ref, coarse_ref, down_ref, up_ref,
               *scratch):
    for n, (row, ref) in enumerate(((0, down_ref), (own_ref.shape[1] - 1, up_ref))):
        attention_row(row, pos_ref, own_ref, other_ref, wqkv_ref, wo_ref, q_ref, k_ref, v_ref, ref, *scratch)
        ref[:, W:] = coarse_ref[:, n * (coarse_ref.shape[1] - 1)]


def inner_body(pos_ref, own_ref, other_ref, wqkv_ref, wo_ref, q_ref, k_ref, v_ref, down_ref, up_ref, *scratch):
    for row, ref in ((1, down_ref), (own_ref.shape[1] - 2, up_ref)):
        attention_row(row, pos_ref, own_ref, other_ref, wqkv_ref, wo_ref, q_ref, k_ref, v_ref, ref, *scratch)


def call(body, name, args, outs, scratch, space=pltpu.VMEM):
    return pl.pallas_call(
        body,
        in_specs=[pl.BlockSpec(memory_space=space)] * len(args),
        out_specs=[pl.BlockSpec(memory_space=pltpu.VMEM)] * len(outs),
        out_shape=[jax.ShapeDtypeStruct(s, t) for s, t in outs],
        scratch_shapes=scratch,
        compiler_params=pltpu.CompilerParams(vmem_limit_bytes=VMEM_LIMIT),
        name=name,
    )(*args)


def own_projections(pos, own, *weights):
    frames, rows = own.shape[:2]
    wide = ((rows, frames, C, W), F32)
    args = [pltpu.with_memory_space_constraint(a, pltpu.HBM) for a in (pos, own, *weights)]
    return call(own_body, "own_projections", args,
                [(pos.shape, F32), (own.shape, BF16), ((3 * C, C), BF16), ((C, C), BF16), wide, wide, wide],
                [pltpu.VMEM((4, C, C), BF16), pltpu.VMEM((frames, C, W), BF16), pltpu.SemaphoreType.DMA((6,))], pltpu.HBM)


def attention(coarse, *args):
    frames = args[1].shape[0]
    if coarse is None:
        body, width, name = inner_body, W, "attention_inner"
    else:
        body, width, name = outer_body, W + HALF, "attention_outer"
        args = args + (coarse,)
    return call(body, name, args, [((frames, width, C), BF16)] * 2,
                [pltpu.VMEM((frames, C, W), BF16), pltpu.VMEM((frames, C, W), F32),
                 pltpu.VMEM((frames, C, W), F32), pltpu.VMEM((frames, C, W), BF16)])


def clear_pads(pad_s):
    for r in range(pad_s.shape[0]):
        pad_s[r, 0:8] = jnp.zeros((8, C), F32)
        pad_s[r, 8 + W:16 + W] = jnp.zeros((8, C), F32)


def shifted(value, pad, out_s, row):
    pad[8:8 + W] = value.astype(F32)
    at = slice(row * W, (row + 1) * W)
    out_s[1, at] = value
    out_s[0, at] = pad[7:7 + W].astype(BF16)
    out_s[2, at] = pad[9:9 + W].astype(BF16)


def taps(source_s, row, w_ref, total=None, steps=(0, 1, 2)):
    for n, dy in enumerate(steps):
        for dx in range(3):
            part = dot(source_s[dx, (row + n) * W:(row + n + 1) * W], w_ref[dy, dx])
            total = part if total is None else total + part
    return total


def relu(value):
    return jnp.maximum(value, jnp.zeros((), value.dtype))


def lift_matrix(flip):
    x = lax.broadcasted_iota(jnp.int32, (W, W), 0)
    at = lax.broadcasted_iota(jnp.int32, (W, W), 1)
    high = at // HALF
    col = at % HALF
    near = x // 2
    far = jnp.clip(near + 2 * (x % 2) - 1, 0, HALF - 1)
    base = 0.75 * (col == near).astype(F32) + 0.25 * (col == far).astype(F32)
    return (base * jnp.where(high == flip, 0.25, 0.75)).astype(BF16)


def stage_one(m0_ref, m1_ref, m2_ref, m3_ref, w1_ref, mid_ref, pad_s, in_s):
    clear_pads(pad_s)

    def frame(f, _):
        for r, ref in enumerate((m0_ref, m1_ref, m2_ref, m3_ref)):
            shifted(relu(ref[f, :W]), pad_s.at[r], in_s, r)
        for j in range(2):
            mid_ref[f, j] = relu(taps(in_s, j, w1_ref)).astype(BF16)
        return 0

    lax.fori_loop(0, m0_ref.shape[0], frame, 0)


def stage_two(above_ref, m0_ref, m1_ref, m2_ref, m3_ref, below_ref, mid_ref, coarse_ref, w1_ref, w2_ref,
              inner_ref, first_ref, second_ref, pad_s, in_s, mid_s, lift_s, coarse_s):
    here = lax.axis_index("space")
    first_edge = here == 0
    last_edge = here == lax.axis_size("space") - 1
    clear_pads(pad_s)
    lift_s[0] = lift_matrix(0)
    lift_s[1] = lift_matrix(1)

    def frame(f, _):
        near, far = coarse_ref[f, 0], coarse_ref[f, 1]
        coarse_s[0:HALF] = jnp.where(first_edge, near, above_ref[f, W:])
        coarse_s[HALF:2 * HALF] = near
        coarse_s[2 * HALF:3 * HALF] = far
        coarse_s[3 * HALF:] = jnp.where(last_edge, far, below_ref[f, W:])
        for r, ref in enumerate((above_ref, m0_ref, m1_ref, m2_ref, m3_ref, below_ref)):
            shifted(relu(ref[f, :W]), pad_s.at[r], in_s, r)
        for j in range(2):
            shifted(mid_ref[f, j], pad_s.at[6 + j], mid_s, j + 1)
        for j in range(2):
            shifted(relu(taps(in_s, 3 * j, w1_ref)).astype(BF16), pad_s.at[8 + j], mid_s, 3 * j)
        for j, steps in enumerate(((1, 2), (0, 1))):
            first_ref[f, j] = taps(in_s, 4 * j, w1_ref, None, steps)
        for j, ref in enumerate((m1_ref, m2_ref)):
            total = taps(mid_s, j, w2_ref, dot(lift_s[1 - j], coarse_s[HALF:3 * HALF]))
            inner_ref[f, j] = (total + ref[f].astype(F32)).astype(BF16)
        for j, (ref, steps) in enumerate(((m0_ref, (1, 2)), (m3_ref, (0, 1)))):
            total = taps(mid_s, 2 * j, w2_ref, dot(lift_s[j], coarse_s[2 * j * HALF:(2 * j + 2) * HALF]), steps)
            second_ref[f, j] = total + ref[f, :W].astype(F32)
        return 0

    lax.fori_loop(0, m0_ref.shape[0], frame, 0)


def stage_three(above_ref, below_ref, inner_ref, first_ref, second_ref, w1_ref, w2_ref, out_ref, pad_s, in_s, mid_s):
    here = lax.axis_index("space")
    edges = (here == 0, here == lax.axis_size("space") - 1)
    clear_pads(pad_s)
    frames = above_ref.shape[0]
    for f in range(frames):
        for j, (ref, edge) in enumerate(zip((above_ref, below_ref), edges)):
            n = 2 * f + j
            step = (2 * j,)
            shifted(relu(ref[f]), pad_s.at[n], in_s, n)
            value = relu(taps(in_s, n, w1_ref, first_ref[f, j], step)).astype(BF16)
            value = jnp.where(edge, jnp.zeros_like(value), value)
            shifted(value, pad_s.at[2 * frames + n], mid_s, n)
            out_ref[f, 3 * j] = taps(mid_s, n, w2_ref, second_ref[f, j], step).astype(BF16)
            out_ref[f, 1 + j] = inner_ref[f, j]


def planes(rows):
    return pltpu.VMEM((3, rows * W, C), BF16)


def pads(rows):
    return pltpu.VMEM((rows, W + 16, C), F32)


def local(fine, coarse, w_query, w_key, w_value, w_out, conv_first, conv_second):
    frames = fine.shape[0]
    size = lax.axis_size("space")
    up = [(i, i + 1) for i in range(size - 1)]
    down = [(i + 1, i) for i in range(size - 1)]
    other = lax.ppermute(fine, "tm", [(0, 1), (1, 0)])
    pos = jnp.asarray(encode_table(2 * frames, C))
    ready = own_projections(pos, fine, w_query, w_key, w_value, w_out)
    held_pos, held, *ready = ready
    m0, m3 = attention(coarse, held_pos, held, other, *ready)
    above = lax.ppermute(m3, "space", up)
    below = lax.ppermute(m0, "space", down)
    m1, m2 = attention(None, held_pos, held, other, *ready)
    above2 = lax.ppermute(m2, "space", up)
    below2 = lax.ppermute(m1, "space", down)
    pair = (frames, 2, W, C)
    (mid,) = call(stage_one, "stage_one", (m0, m1, m2, m3, conv_first), [(pair, BF16)], [pads(4), planes(4)])
    inner, first, second = call(
        stage_two, "stage_two", (above, m0, m1, m2, m3, below, mid, coarse, conv_first, conv_second),
        [(pair, BF16), (pair, F32), (pair, F32)],
        [pads(10), planes(6), planes(4), pltpu.VMEM((2, W, W), BF16), pltpu.VMEM((4 * HALF, C), BF16)])
    (out,) = call(stage_three, "stage_three", (above2, below2, inner, first, second, conv_first, conv_second),
                  [((frames, 4, W, C), BF16)], [pads(4 * frames), planes(2 * frames), planes(2 * frames)])
    return out


def solution(mesh):
    split = P("tm", "space", None, None)
    return jax.shard_map(
        local,
        mesh=mesh,
        in_specs=(split, split, P(), P(), P(), P(), P(), P()),
        out_specs=split,
        check_vma=False,
    )
```

time: 90.1 us -> 55.2 us (0.61)
  waiting for transfers between devices: 24.7 us -> 6.64 us
  Pallas kernels: 42.4 us -> 32.4 us
  local copies, waits for them, and re-layouts: 4.5 us -> 0.02 us
  other arithmetic: 2.67 us -> 0 us
    ppermute x4, waiting for transfers between devices: 24.1 us -> 6.63 us  [the longest x1 5.85 us: local(): below = lax.ppermute(m0, 'space', down)]
    pallas_call x2 -> x6, Pallas kernels: 42.4 us -> 32.4 us  [call(): pl.pallas_call(body, in_specs=[pl.BlockSpec(memory_space=space)] * len(ar...]
    unnamed x12 -> x6, local copies, waits for them, and re-layouts: 2.71 us -> 0.02 us
    select_n x1 -> x0, other arithmetic: 2 us -> none  [local(): pos = jnp.where(tm == 0, table, jnp.roll(table, frames, axis=0))]
    broadcast_in_dim x2 -> x0, local copies, waits for them, and re-layouts: 1.75 us -> none  [local(): jnp.broadcast_to(jnp.asarray(encode_table(2 * frames, C))[:, :, None], (2...]
  transfers between devices with their start and end apart: 5 -> 5, of which waited for: 3 -> 2; matrix products, arithmetic and copies ran while one was open for 5% -> 0% of each run, Pallas kernels for 0% -> 43%
where the time goes in v1:
time: 55.2 us; the launch traced here: 55 us
  Pallas kernels  32.4 us (59%)
  starting transfers between devices  15.8 us (29%)
  waiting for transfers between devices  6.64 us (12%)
    pallas_call x6, Pallas kernels, call(): pl.pallas_call(body, in_specs=[pl.BlockSpec(memory_space=space)] * len(ar...  32.4 us
    ppermute x1, starting transfers between devices, local(): above2 = lax.ppermute(m2, 'space', up)  7.61 us
    ppermute x1, waiting for transfers between devices, local(): below = lax.ppermute(m0, 'space', down)  5.85 us
    ppermute x1, starting transfers between devices, local(): above = lax.ppermute(m3, 'space', up)  3.39 us
    ppermute x1, starting transfers between devices, local(): below = lax.ppermute(m0, 'space', down)  2.58 us
    ppermute x1, starting transfers between devices, local(): below2 = lax.ppermute(m1, 'space', down)  2.23 us
  transfers between devices with their start and end apart: 5, of which 2 were waited for; matrix products, arithmetic and copies ran while one was open for 0% of the time, Pallas kernels for 43%

profile of v1, /device:TPU:30, one launch (start us, length us, event | category | flops | bytes accessed | tf_op | source)
XLA Modules:
  0.0 55.0 jit_solution(4257009734362182517)
XLA Ops:
  0.0 0.0 copy-start.2
  0.0 0.0 collective-permute-start
  0.0 5.7 %own_projections.1 = (f32[8,256,128]{2,1,0:T(8,128)S(1)}, bf16[4,4,256,256]{3,2,1,0:T(8,128)(2,1)S(1)}, bf16[768,256]{1,0:T(8,128)(2,1)S(1)}, bf16[256,256]{1,0:...) custom-call(f32[8,256,128]{2,1,0:T(8,128)} %constant.2.clone.pos_hbm, ...), custom_call_target="tpu_custom_call" | custom-call | tf_op jit(solution)/shard_map/own_projections/pallas_call | solution.py:145
  5.7 0.0 collective-permute-done.other_ref
  5.7 0.0 copy-done.2
  5.7 5.2 %attention_outer.1 = (bf16[4,384,256]{2,1,0:T(8,128)(2,1)S(1)}, bf16[4,384,256]{2,1,0:T(8,128)(2,1)S(1)}) custom-call(f32[8,256,128]{2,1,0:T(8,128)S(1)} %get-tuple-element.19.pos_ref, bf16[4,4,256,256]{3,2,1,0:T(8,128)(2,1)S(1)} %get-tuple-element.20.own_ref, bf16[4,4,256,256]{3,2,1,0:T(8,128)(2,1)S(1)} %collective-permute-done.other_ref, ...), custom_call_target="tpu_custom_call" | custom-call | tf_op jit(solution)/shard_map/attention_outer/pallas_call | solution.py:145
  10.9 3.4 %collective-permute-start.3 = (bf16[4,384,256]{2,1,0:T(8,128)(2,1)S(1)}, bf16[4,384,256]{2,1,0:T(8,128)(2,1)S(1)}, u32[]{:S(2)}, u32[]{:S(2)}) collective-permute-start(bf16[4,384,256]{2,1,0:T(8,128)(2,1)S(1)} %get-tuple-element.28.m3_ref), channel_id=1, source_target_pairs={{0,1},{1,2},{2,3},{3,4},{4,5},{5,6},{6,7},{7,8},{8,9},{9,10},{10,1... | collective-permute-start | bytes 2359304 | tf_op jit(solution)/shard_map/ppermute | solution.py:296
  14.3 0.0 copy-start
  14.3 2.6 %collective-permute-start.4 = (bf16[4,384,256]{2,1,0:T(8,128)(2,1)S(1)}, bf16[4,384,256]{2,1,0:T(8,128)(2,1)S(1)}, u32[]{:S(2)}, u32[]{:S(2)}) collective-permute-start(bf16[4,384,256]{2,1,0:T(8,128)(2,1)S(1)} %get-tuple-element.29.m0_ref), channel_id=1, source_target_pairs={{1,0},{2,1},{3,2},{4,3},{5,4},{6,5},{7,6},{8,7},{9,8},{10,9},{11,1... | collective-permute-start | bytes 2359304 | tf_op jit(solution)/shard_map/ppermute | solution.py:297
  16.9 5.1 %attention_inner.1 = (bf16[4,256,256]{2,1,0:T(8,128)(2,1)S(1)}, bf16[4,256,256]{2,1,0:T(8,128)(2,1)S(1)}) custom-call(f32[8,256,128]{2,1,0:T(8,128)S(1)} %get-tuple-element.19.pos_ref, bf16[4,4,256,256]{3,2,1,0:T(8,128)(2,1)S(1)} %get-tuple-element.20.own_ref, bf16[4,4,256,256]{3,2,1,0:T(8,128)(2,1)S(1)} %collective-permute-done.other_ref, ...), custom_call_target="tpu_custom_call" | custom-call | tf_op jit(solution)/shard_map/attention_inner/pallas_call | solution.py:145
  22.1 7.6 %collective-permute-start.1 = (bf16[4,256,256]{2,1,0:T(8,128)(2,1)S(1)}, bf16[4,256,256]{2,1,0:T(8,128)(2,1)S(1)}, u32[]{:S(2)}, u32[]{:S(2)}) collective-permute-start(bf16[4,256,256]{2,1,0:T(8,128)(2,1)S(1)} %get-tuple-element.26.m2_ref), channel_id=1, source_target_pairs={{0,1},{1,2},{2,3},{3,4},{4,5},{5,6},{6,7},{7,8},{8,9},{9,10},{10,1... | collective-permute-start | bytes 1572872 | tf_op jit(solution)/shard_map/ppermute | solution.py:299
  29.7 0.0 copy-start.1
  29.7 2.2 %collective-permute-start.2 = (bf16[4,256,256]{2,1,0:T(8,128)(2,1)S(1)}, bf16[4,256,256]{2,1,0:T(8,128)(2,1)S(1)}, u32[]{:S(2)}, u32[]{:S(2)}) collective-permute-start(bf16[4,256,256]{2,1,0:T(8,128)(2,1)S(1)} %get-tuple-element.27.m1_ref), channel_id=1, source_target_pairs={{1,0},{2,1},{3,2},{4,3},{5,4},{6,5},{7,6},{8,7},{9,8},{10,9},{11,1... | collective-permute-start | bytes 1572872 | tf_op jit(solution)/shard_map/ppermute | solution.py:300
  31.9 0.0 copy-done
  31.9 3.2 %stage_one.1.mid_ref = bf16[4,2,256,256]{3,2,1,0:T(8,128)(2,1)S(1)} custom-call(bf16[4,384,256]{2,1,0:T(8,128)(2,1)S(1)} %get-tuple-element.29.m0_ref, bf16[4,256,256]{2,1,0:T(8,128)(2,1)S(1)} %get-tuple-element.27.m1_ref, bf16[4,256,256]{2,1,0:T(8,128)(2,1)S(1)} %get-tuple-element.26.m2_ref, bf16[4,384,256]{2,1,0:T(8,128)(2,1)S(1)} %get-tuple-element.28.m3_ref, ...), custom_call_target="tpu_custom_call" | custom-call | tf_op jit(solution)/shard_map/stage_one/pallas_call | solution.py:145
  35.1 0.0 collective-permute-done.3.above_ref
  35.1 5.8 %collective-permute-done.4.below_ref = bf16[4,384,256]{2,1,0:T(8,128)(2,1)S(1)} collective-permute-done((bf16[4,384,256]{2,1,0:T(8,128)(2,1)S(1)}, bf16[4,384,256]{2,1,0:T(8,128)(2,1)S(1)}, u32[]{:S(2)}, u32[]{:S(2)}) %collective-permute-start.4) | collective-permute-done | bytes 786464 | tf_op jit(solution)/shard_map/ppermute | solution.py:297
  41.0 0.0 copy-done.1
  41.0 9.6 %stage_two.1 = (bf16[4,2,256,256]{3,2,1,0:T(8,128)(2,1)S(1)}, f32[4,2,256,256]{3,2,1,0:T(8,128)S(1)}, f32[4,2,256,256]{3,2,1,0:T(8,128)S(1)}) custom-call(bf16[4,384,256]{2,1,0:T(8,128)(2,1)S(1)} %collective-permute-done.3.above_ref, bf16[4,384,256]{2,1,0:T(8,128)(2,1)S(1)} %get-tuple-element.29.m0_ref, bf16[4,256,256]{2,1,0:T(8,128)(2,1)S(1)} %get-tuple-element.27.m1_ref, ...), custom_call_target="tpu_custom_call" | custom-call | tf_op jit(solution)/shard_map/stage_two/pallas_call | solution.py:145
  50.6 0.0 collective-permute-done.1.above_ref
  50.6 0.8 %collective-permute-done.2.below_ref = bf16[4,256,256]{2,1,0:T(8,128)(2,1)S(1)} collective-permute-done((bf16[4,256,256]{2,1,0:T(8,128)(2,1)S(1)}, bf16[4,256,256]{2,1,0:T(8,128)(2,1)S(1)}, u32[]{:S(2)}, u32[]{:S(2)}) %collective-permute-start.2) | collective-permute-done | bytes 524320 | tf_op jit(solution)/shard_map/ppermute | solution.py:300
  51.4 3.6 %stage_three.1 = bf16[4,4,256,256]{3,2,1,0:T(8,128)(2,1)} custom-call(bf16[4,256,256]{2,1,0:T(8,128)(2,1)S(1)} %collective-permute-done.1.above_ref, bf16[4,256,256]{2,1,0:T(8,128)(2,1)S(1)} %collective-permute-done.2.below_ref, bf16[4,2,256,256]{3,2,1,0:T(8,128)(2,1)S(1)} %get-tuple-element.30.inner_ref, ...), custom_call_target="tpu_custom_call" | custom-call | tf_op jit(solution)/shard_map/stage_three/pallas_call | solution.py:145
Async XLA Ops:
  0.0 5.7 %copy-start.2 = (bf16[4,2,128,256]{3,2,1,0:T(8,128)(2,1)S(1)}, bf16[4,2,128,256]{3,2,1,0:T(8,128)(2,1)}, u32[]{:S(2)}) copy-start(bf16[4,2,128,256]{3,2,1,0:T(8,128)(2,1)} %coarse_ref.3) | copy-start | bytes 1572868
  0.0 5.7 %collective-permute-start = (bf16[4,4,256,256]{3,2,1,0:T(8,128)(2,1)}, bf16[4,4,256,256]{3,2,1,0:T(8,128)(2,1)S(1)}, u32[]{:S(2)}, u32[]{:S(2)}) collective-permute-start(bf16[4,4,256,256]{3,2,1,0:T(8,128)(2,1)} %own_hbm.1), channel_id=1, source_target_pairs={{0,64},{64,0},{1,65},{65,1},{2,66},{66,2},{3,67},{67,3},{4,68},{68... | collective-permute-start | bytes 6291464 | tf_op jit(solution)/shard_map/ppermute | solution.py:291
  10.9 24.2 %collective-permute-start.3 = (bf16[4,384,256]{2,1,0:T(8,128)(2,1)S(1)}, bf16[4,384,256]{2,1,0:T(8,128)(2,1)S(1)}, u32[]{:S(2)}, u32[]{:S(2)}) collective-permute-start(bf16[4,384,256]{2,1,0:T(8,128)(2,1)S(1)} %get-tuple-element.28.m3_ref), channel_id=1, source_target_pairs={{0,1},{1,2},{2,3},{3,4},{4,5},{5,6},{6,7},{7,8},{8,9},{9,10},{10,1... | collective-permute-start | bytes 2359304 | tf_op jit(solution)/shard_map/ppermute | solution.py:296
  14.3 17.6 %copy-start = (bf16[3,3,256,256]{3,2,1,0:T(8,128)(2,1)S(1)}, bf16[3,3,256,256]{3,2,1,0:T(8,128)(2,1)}, u32[]{:S(2)}) copy-start(bf16[3,3,256,256]{3,2,1,0:T(8,128)(2,1)} %w1_ref.5) | copy-start | bytes 3538948
  14.3 26.7 %collective-permute-start.4 = (bf16[4,384,256]{2,1,0:T(8,128)(2,1)S(1)}, bf16[4,384,256]{2,1,0:T(8,128)(2,1)S(1)}, u32[]{:S(2)}, u32[]{:S(2)}) collective-permute-start(bf16[4,384,256]{2,1,0:T(8,128)(2,1)S(1)} %get-tuple-element.29.m0_ref), channel_id=1, source_target_pairs={{1,0},{2,1},{3,2},{4,3},{5,4},{6,5},{7,6},{8,7},{9,8},{10,9},{11,1... | collective-permute-start | bytes 2359304 | tf_op jit(solution)/shard_map/ppermute | solution.py:297
  22.1 28.6 %collective-permute-start.1 = (bf16[4,256,256]{2,1,0:T(8,128)(2,1)S(1)}, bf16[4,256,256]{2,1,0:T(8,128)(2,1)S(1)}, u32[]{:S(2)}, u32[]{:S(2)}) collective-permute-start(bf16[4,256,256]{2,1,0:T(8,128)(2,1)S(1)} %get-tuple-element.26.m2_ref), channel_id=1, source_target_pairs={{0,1},{1,2},{2,3},{3,4},{4,5},{5,6},{6,7},{7,8},{8,9},{9,10},{10,1... | collective-permute-start | bytes 1572872 | tf_op jit(solution)/shard_map/ppermute | solution.py:299
  29.7 11.3 %copy-start.1 = (bf16[3,3,256,256]{3,2,1,0:T(8,128)(2,1)S(1)}, bf16[3,3,256,256]{3,2,1,0:T(8,128)(2,1)}, u32[]{:S(2)}) copy-start(bf16[3,3,256,256]{3,2,1,0:T(8,128)(2,1)} %w2_ref.3) | copy-start | bytes 3538948
  29.7 21.7 %collective-permute-start.2 = (bf16[4,256,256]{2,1,0:T(8,128)(2,1)S(1)}, bf16[4,256,256]{2,1,0:T(8,128)(2,1)S(1)}, u32[]{:S(2)}, u32[]{:S(2)}) collective-permute-start(bf16[4,256,256]{2,1,0:T(8,128)(2,1)S(1)} %get-tuple-element.27.m1_ref), channel_id=1, source_target_pairs={{1,0},{2,1},{3,2},{4,3},{5,4},{6,5},{7,6},{8,7},{9,8},{10,9},{11,1... | collective-permute-start | bytes 1572872 | tf_op jit(solution)/shard_map/ppermute | solution.py:300

commit v2 on v1

v2 whole, which is shorter than its diff:
```python
import functools

import jax
import jax.numpy as jnp
import numpy as np
from jax import lax
from jax.experimental import pallas as pl
from jax.experimental.pallas import tpu as pltpu
from jax.sharding import PartitionSpec as P

HEADS = 8
C = 256
D = C // HEADS
W = 256
HALF = W // 2
F32 = jnp.float32
BF16 = jnp.bfloat16
VMEM_LIMIT = 20 * 1024 * 1024


def encode_table(frames, width):
    half = width // 2
    inverse = np.exp(-np.log(10000.0) * 2.0 * np.arange(half) / width)
    angles = np.arange(frames)[:, None] * inverse[None, :]
    table = np.concatenate([np.sin(angles), np.cos(angles)], axis=1).astype(np.float32)
    return np.ascontiguousarray(np.broadcast_to(table[:, :, None], (frames, width, 128)))


def dot(a, b):
    return jnp.dot(a, b, preferred_element_type=F32)


def normed_row(x_ref, i, row, pos, norm):
    for half in range(W // 128):
        lanes = slice(half * 128, half * 128 + 128)
        h = x_ref[i, row, lanes, :].T.astype(F32) + pos
        center = h - jnp.sum(h, axis=0, keepdims=True) * (1.0 / C)
        spread = jnp.sum(center * center, axis=0, keepdims=True) * (1.0 / C)
        norm[:, lanes] = (center * lax.rsqrt(spread + 1e-05)).astype(BF16)


def own_row(at_row, row, pos_ref, own_ref, wqkv_ref, q_ref, k_ref, v_ref, norm_s):
    frames = own_ref.shape[0]
    base = lax.axis_index("tm") * frames
    for f in range(frames):
        normed_row(own_ref, f, row, pos_ref[base + f], norm_s.at[f])
        y = dot(wqkv_ref[...], norm_s[f])
        q_ref[at_row, f] = y[:C]
        k_ref[at_row, f] = y[C:2 * C]
        v_ref[at_row, f] = y[2 * C:]


def attention_row(at_row, row, pos_ref, own_ref, other_ref, wkv_ref, wo_ref, q_ref, ko_ref, vo_ref, out_ref,
                  norm_s, k_s, v_s, att_s):
    frames = own_ref.shape[0]
    keys = 2 * frames
    base = (1 - lax.axis_index("tm")) * frames

    for f in range(frames):
        normed_row(other_ref, f, row, pos_ref[base + f], norm_s.at[f])
        y = dot(wkv_ref[C:], norm_s[f])
        k_s[f] = y[:C]
        v_s[f] = y[C:]

    factor = float(np.log2(np.e) / np.sqrt(D))
    for half in range(W // 128):
        lanes = slice(half * 128, half * 128 + 128)

        def score(d, acc):
            at = pl.ds(pl.multiple_of(d * HEADS, HEADS), HEADS)
            qs = [q_ref[at_row, a, at, lanes] for a in range(frames)]
            ks = [ko_ref[at_row, b, at, lanes] for b in range(frames)] + [k_s[b, at, lanes] for b in range(frames)]
            return tuple(acc[a * keys + b] + qs[a] * ks[b] for a in range(frames) for b in range(keys))

        zero = jnp.zeros((HEADS, 128), F32)
        acc = lax.fori_loop(0, D, score, (zero,) * (frames * keys), unroll=4)
        weights = []
        for a in range(frames):
            line = acc[a * keys:(a + 1) * keys]
            top = line[0]
            for s in line[1:]:
                top = jnp.maximum(top, s)
            powers = [jnp.exp2((s - top) * factor) for s in line]
            total = powers[0]
            for p in powers[1:]:
                total = total + p
            inv = 1.0 / total
            weights += [p * inv for p in powers]

        def gather(d2, _):
            outs = [[] for _ in range(frames)]
            for sub in range(2):
                at = pl.ds(pl.multiple_of(d2 * 2 * HEADS + sub * HEADS, HEADS), HEADS)
                vs = [vo_ref[at_row, b, at, lanes] for b in range(frames)] + [v_s[b, at, lanes] for b in range(frames)]
                for a in range(frames):
                    total = weights[a * keys] * vs[0]
                    for b in range(1, keys):
                        total = total + weights[a * keys + b] * vs[b]
                    outs[a].append(total)
            at = pl.ds(pl.multiple_of(d2 * 2 * HEADS, 2 * HEADS), 2 * HEADS)
            for a in range(frames):
                att_s[a, at, lanes] = jnp.concatenate(outs[a], axis=0).astype(BF16)
            return 0

        lax.fori_loop(0, D // 2, gather, 0, unroll=2)

    for a in range(frames):
        branch = lax.dot_general(att_s[a], wo_ref[...], (((0,), (0,)), ((), ())), preferred_element_type=F32)
        out_ref[a, :W] = (own_ref[a, row].astype(F32) + branch).astype(BF16)


def own_body(pos_hbm, own_hbm, wq_hbm, wk_hbm, wv_hbm, wo_hbm,
             pos_ref, own_ref, wqkv_ref, wor_ref, q_ref, k_ref, v_ref, w_s, norm_s, sems):
    frames, rows = own_hbm.shape[:2]
    loads = [pltpu.make_async_copy(ref, w_s.at[n], sems.at[n]) for n, ref in enumerate((wq_hbm, wk_hbm, wv_hbm, wo_hbm))]
    loads.append(pltpu.make_async_copy(pos_hbm, pos_ref, sems.at[4]))
    loads.append(pltpu.make_async_copy(own_hbm, own_ref, sems.at[5]))
    for load in loads:
        load.start()
    to = lax.broadcasted_iota(jnp.int32, (C, C), 0)
    at = lax.broadcasted_iota(jnp.int32, (C, C), 1)
    pick = (at == (to % HEADS) * D + to // HEADS).astype(BF16)
    nt = (((1,), (1,)), ((), ()))
    for load in loads[:4]:
        load.wait()
    for n in range(3):
        wqkv_ref[n * C:(n + 1) * C] = lax.dot_general(pick, w_s[n], nt, preferred_element_type=F32).astype(BF16)
    wor_ref[...] = dot(pick, w_s[3]).astype(BF16)
    for load in loads[4:]:
        load.wait()
    for n, row in enumerate((0, own_ref.shape[1] - 1)):
        own_row(n, row, pos_ref, own_ref, wqkv_ref, q_ref, k_ref, v_ref, norm_s)


def outer_body(pos_ref, own_ref, other_ref, wqkv_ref, wo_ref, q_ref, k_ref, v_ref, coarse_ref, down_ref, up_ref,
               norm_s, k_s, v_s, att_s):
    for n, (row, ref) in enumerate(((0, down_ref), (own_ref.shape[1] - 1, up_ref))):
        attention_row(n, row, pos_ref, own_ref, other_ref, wqkv_ref, wo_ref, q_ref, k_ref, v_ref, ref,
                      norm_s, k_s, v_s, att_s)
        ref[:, W:] = coarse_ref[:, n * (coarse_ref.shape[1] - 1)]


def inner_body(pos_ref, own_ref, other_ref, wqkv_ref, wo_ref, before_ref, down_ref, up_ref,
               norm_s, k_s, v_s, att_s, q_s, ko_s, vo_s):
    del before_ref
    for row, ref in ((1, down_ref), (own_ref.shape[1] - 2, up_ref)):
        own_row(0, row, pos_ref, own_ref, wqkv_ref, q_s, ko_s, vo_s, norm_s)
        attention_row(0, row, pos_ref, own_ref, other_ref, wqkv_ref, wo_ref, q_s, ko_s, vo_s, ref,
                      norm_s, k_s, v_s, att_s)


def call(body, name, args, outs, scratch, micros, space=pltpu.VMEM):
    return pl.pallas_call(
        body,
        in_specs=[pl.BlockSpec(memory_space=space)] * len(args),
        out_specs=[pl.BlockSpec(memory_space=pltpu.VMEM)] * len(outs),
        out_shape=[jax.ShapeDtypeStruct(s, t) for s, t in outs],
        scratch_shapes=scratch,
        compiler_params=pltpu.CompilerParams(vmem_limit_bytes=VMEM_LIMIT),
        cost_estimate=pl.CostEstimate(flops=micros * 10**9, transcendentals=0, bytes_accessed=1 << 20),
        name=name,
    )(*args)


def own_projections(pos, own, *weights):
    frames, rows = own.shape[:2]
    wide = ((2, frames, C, W), F32)
    args = [pltpu.with_memory_space_constraint(a, pltpu.HBM) for a in (pos, own, *weights)]
    return call(own_body, "own_projections", args,
                [(pos.shape, F32), (own.shape, BF16), ((3 * C, C), BF16), ((C, C), BF16), wide, wide, wide],
                [pltpu.VMEM((4, C, C), BF16), pltpu.VMEM((frames, C, W), BF16), pltpu.SemaphoreType.DMA((6,))], 6, pltpu.HBM)


def attention(body, name, args, width, extra, micros):
    frames = args[1].shape[0]
    return call(body, name, args, [((frames, width, C), BF16)] * 2,
                [pltpu.VMEM((frames, C, W), BF16), pltpu.VMEM((frames, C, W), F32),
                 pltpu.VMEM((frames, C, W), F32), pltpu.VMEM((frames, C, W), BF16)] + extra, micros)


def clear_pads(pad_s):
    for r in range(pad_s.shape[0]):
        pad_s[r, 0:8] = jnp.zeros((8, C), F32)
        pad_s[r, 8 + W:16 + W] = jnp.zeros((8, C), F32)


def shifted(value, pad, out_s, row):
    pad[8:8 + W] = value.astype(F32)
    at = slice(row * W, (row + 1) * W)
    out_s[1, at] = value
    out_s[0, at] = pad[7:7 + W].astype(BF16)
    out_s[2, at] = pad[9:9 + W].astype(BF16)


def taps(source_s, row, w_ref, total=None, steps=(0, 1, 2)):
    for n, dy in enumerate(steps):
        for dx in range(3):
            part = dot(source_s[dx, (row + n) * W:(row + n + 1) * W], w_ref[dy, dx])
            total = part if total is None else total + part
    return total


def relu(value):
    return jnp.maximum(value, jnp.zeros((), value.dtype))


def lift_matrices():
    x, at = np.indices((W, W))
    col = at % HALF
    near = x // 2
    far = np.clip(near + 2 * (x % 2) - 1, 0, HALF - 1)
    base = 0.75 * (col == near) + 0.25 * (col == far)
    second = at // HALF == 1
    return np.stack([base * np.where(second, 0.75, 0.25), base * np.where(second, 0.25, 0.75)]).astype(np.float32)


def stage_one(m0_ref, m1_ref, m2_ref, m3_ref, w1_ref, mid_ref, pad_s, in_s):
    clear_pads(pad_s)

    def frame(f, _):
        for r, ref in enumerate((m0_ref, m1_ref, m2_ref, m3_ref)):
            shifted(relu(ref[f, :W]), pad_s.at[r], in_s, r)
        for j in range(2):
            mid_ref[f, j] = relu(taps(in_s, j, w1_ref)).astype(BF16)
        return 0

    lax.fori_loop(0, m0_ref.shape[0], frame, 0)


def stage_two(side, halo_ref, near_ref, far_ref, mid_ref, coarse_ref, lift_ref, w1_ref, w2_ref,
              inner_ref, first_ref, second_ref, pad_s, in_s, mid_s, coarse_s):
    edge = lax.axis_index("space") == side * (lax.axis_size("space") - 1)
    steps = (0, 1) if side else (1, 2)
    order = 1 - 2 * side
    clear_pads(pad_s)

    def frame(f, _):
        own = coarse_ref[f, side]
        coarse_s[side * HALF:(side + 1) * HALF] = jnp.where(edge, own, halo_ref[f, W:])
        coarse_s[(1 - side) * HALF:(2 - side) * HALF] = own
        for r, ref in enumerate((halo_ref, near_ref, far_ref)[::order]):
            shifted(relu(ref[f, :W]), pad_s.at[r], in_s, r)
        for j in range(2):
            shifted(mid_ref[f, j], pad_s.at[3 + j], mid_s, j + 1 - side)
        shifted(relu(taps(in_s, 0, w1_ref)).astype(BF16), pad_s.at[5], mid_s, 2 * side)
        first_ref[f] = taps(in_s, side, w1_ref, None, steps)
        total = taps(mid_s, 0, w2_ref, dot(lift_ref[1 - side], coarse_ref[f].reshape(2 * HALF, C)))
        inner_ref[f] = (total + far_ref[f, :W].astype(F32)).astype(BF16)
        total = taps(mid_s, side, w2_ref, dot(lift_ref[side], coarse_s[...]), steps)
        second_ref[f] = total + near_ref[f, :W].astype(F32)
        return 0

    lax.fori_loop(0, near_ref.shape[0], frame, 0)


def stage_three(side, halo_ref, inner_ref, first_ref, second_ref, w1_ref, w2_ref, *rest):
    out_hbm, pad_s, in_s, mid_s, row_s, sems = rest[-6:]
    edge = lax.axis_index("space") == side * (lax.axis_size("space") - 1)
    frames = halo_ref.shape[0]
    copies = [pltpu.make_async_copy(inner_ref.at[f], out_hbm.at[f, 1 + side], sems.at[f]) for f in range(frames)]
    copies += [pltpu.make_async_copy(row_s.at[f], out_hbm.at[f, 3 * side], sems.at[frames + f]) for f in range(frames)]
    for copy in copies[:frames]:
        copy.start()
    clear_pads(pad_s)
    step = (2 * side,)
    for f in range(frames):
        shifted(relu(halo_ref[f]), pad_s.at[f], in_s, f)
        value = relu(taps(in_s, f, w1_ref, first_ref[f], step)).astype(BF16)
        value = jnp.where(edge, jnp.zeros_like(value), value)
        shifted(value, pad_s.at[frames + f], mid_s, f)
        row_s[f] = taps(mid_s, f, w2_ref, second_ref[f], step).astype(BF16)
        copies[frames + f].start()
    for copy in copies:
        copy.wait()


def last_stage(side, name, args, out, rows):
    frames = args[0].shape[0]
    before = [] if out is None else [out]
    return pl.pallas_call(
        functools.partial(stage_three, side),
        in_specs=[pl.BlockSpec(memory_space=pltpu.VMEM)] * len(args)
        + [pl.BlockSpec(memory_space=pltpu.HBM)] * len(before),
        out_specs=pl.BlockSpec(memory_space=pltpu.HBM),
        out_shape=jax.ShapeDtypeStruct((frames, rows, W, C), BF16),
        scratch_shapes=[pads(2 * frames), planes(frames), planes(frames), pltpu.VMEM((frames, W, C), BF16),
                        pltpu.SemaphoreType.DMA((2 * frames,))],
        input_output_aliases={len(args): 0} if before else {},
        compiler_params=pltpu.CompilerParams(vmem_limit_bytes=VMEM_LIMIT),
        cost_estimate=pl.CostEstimate(flops=2 * 10**9, transcendentals=0, bytes_accessed=1 << 20),
        name=name,
    )(*args, *before)


def planes(rows):
    return pltpu.VMEM((3, rows * W, C), BF16)


def pads(rows):
    return pltpu.VMEM((rows, W + 16, C), F32)


def local(fine, coarse, w_query, w_key, w_value, w_out, conv_first, conv_second):
    frames = fine.shape[0]
    size = lax.axis_size("space")
    up = [(i, i + 1) for i in range(size - 1)]
    down = [(i + 1, i) for i in range(size - 1)]
    other = lax.ppermute(fine, "tm", [(0, 1), (1, 0)])
    pos = jnp.asarray(encode_table(2 * frames, C))
    ready = own_projections(pos, fine, w_query, w_key, w_value, w_out)
    held_pos, held, wqkv, wo, q, k, v = ready
    m0, m3 = attention(outer_body, "attention_outer", (held_pos, held, other, wqkv, wo, q, k, v, coarse), W + HALF,
                       [], 5)
    above = lax.ppermute(m3, "space", up)
    below = lax.ppermute(m0, "space", down)
    wide = pltpu.VMEM((1, frames, C, W), F32)
    m1, m2 = attention(inner_body, "attention_inner", (held_pos, held, other, wqkv, wo, m0), W, [wide] * 3, 7)
    above2 = lax.ppermute(m2, "space", up)
    below2 = lax.ppermute(m1, "space", down)
    (mid,) = call(stage_one, "stage_one", (m0, m1, m2, m3, conv_first), [((frames, 2, W, C), BF16)],
                  [pads(4), planes(4)], 3)
    row = (frames, W, C)
    lift = jnp.asarray(lift_matrices(), BF16)
    parts = []
    for side, (halo, near, far) in enumerate(((above, m0, m1), (below, m3, m2))):
        parts.append(call(functools.partial(stage_two, side), "stage_two_%d" % side,
                          (halo, near, far, mid, coarse, lift, conv_first, conv_second),
                          [(row, BF16), (row, F32), (row, F32)],
                          [pads(6), planes(3), planes(3), pltpu.VMEM((2 * HALF, C), BF16)], 5))
    out = None
    for side, halo in enumerate((above2, below2)):
        out = last_stage(side, "stage_three_%d" % side, (halo, *parts[side], conv_first, conv_second, parts[1 - side][0]),
                         out, fine.shape[1])
    return out


def solution(mesh):
    split = P("tm", "space", None, None)
    return jax.shard_map(
        local,
        mesh=mesh,
        in_specs=(split, split, P(), P(), P(), P(), P(), P()),
        out_specs=split,
        check_vma=False,
    )
```

time: 55.2 us -> 52.4 us (0.949)
  waiting for transfers between devices: 6.64 us -> 1.95 us
  Pallas kernels: 32.4 us -> 33.3 us
  starting transfers between devices: 15.8 us -> 16.4 us
    ppermute x1, waiting for transfers between devices: 5.85 us -> 0.01 us  [local(): below = lax.ppermute(m0, 'space', down)]
    pallas_call x0 -> x2, Pallas kernels: none -> 4.06 us  [last_stage(): pl.pallas_call(functools.partial(stage_three, side), in_specs=[pl.BlockSp...]
    pallas_call x6, Pallas kernels: 32.4 us -> 29.2 us  [call(): pl.pallas_call(body, in_specs=[pl.BlockSpec(memory_space=space)] * len(ar...]
    ppermute x1, waiting for transfers between devices: 0.01 us -> 0.77 us  [local(): other = lax.ppermute(fine, 'tm', [(0, 1), (1, 0)])]
  transfers between devices with their start and end apart: 5 -> 5, of which waited for: 2 -> 2; matrix products, arithmetic and copies ran while one was open for 0% -> 0% of each run, Pallas kernels for 43% -> 50%
where the time goes in v2:
time: 52.4 us; the launch traced here: 51.9 us
  Pallas kernels  33.3 us (64%)
  starting transfers between devices  16.4 us (31%)
  waiting for transfers between devices  1.95 us (4%)
    pallas_call x6, Pallas kernels, call(): pl.pallas_call(body, in_specs=[pl.BlockSpec(memory_space=space)] * len(ar...  29.2 us
    ppermute x1, starting transfers between devices, local(): above2 = lax.ppermute(m2, 'space', up)  7.63 us
    pallas_call x2, Pallas kernels, last_stage(): pl.pallas_call(functools.partial(stage_three, side), in_specs=[pl.BlockSp...  4.06 us
    ppermute x1, starting transfers between devices, local(): above = lax.ppermute(m3, 'space', up)  3.4 us
    ppermute x1, starting transfers between devices, local(): below2 = lax.ppermute(m1, 'space', down)  2.74 us
    ppermute x1, starting transfers between devices, local(): below = lax.ppermute(m0, 'space', down)  2.57 us
    ppermute x1, waiting for transfers between devices, local(): below2 = lax.ppermute(m1, 'space', down)  1.18 us
  transfers between devices with their start and end apart: 5, of which 2 were waited for; matrix products, arithmetic and copies ran while one was open for 0% of the time, Pallas kernels for 50%

profile of v2, /device:TPU:30, one launch (start us, length us, event | category | flops | bytes accessed | tf_op | source)
XLA Modules:
  0.0 51.9 jit_solution(13696948630996601686)
XLA Ops:
  0.0 0.0 copy-start.2
  0.0 0.0 collective-permute-start
  0.0 3.6 %own_projections.1 = (f32[8,256,128]{2,1,0:T(8,128)S(1)}, bf16[4,4,256,256]{3,2,1,0:T(8,128)(2,1)S(1)}, bf16[768,256]{1,0:T(8,128)(2,1)S(1)}, bf16[256,256]{1,0:...) custom-call(f32[8,256,128]{2,1,0:T(8,128)} %constant.4.clone.pos_hbm, ...), custom_call_target="tpu_custom_call" | custom-call | flops 6000000000 | bytes 1048576 | tf_op jit(solution)/shard_map/own_projections/pallas_call | solution.py:153
  3.6 0.8 %collective-permute-done.other_ref = bf16[4,4,256,256]{3,2,1,0:T(8,128)(2,1)S(1)} collective-permute-done((bf16[4,4,256,256]{3,2,1,0:T(8,128)(2,1)}, bf16[4,4,256,256]{3,2,1,0:T(8,128)(2,1)S(1)}, u32[]{:S(2)}, u32[]{:S(2)}) %collective-permute-start) | collective-permute-done | bytes 2097184 | tf_op jit(solution)/shard_map/ppermute | solution.py:308
  4.4 0.0 copy-done.2
  4.4 5.2 %attention_outer.1 = (bf16[4,384,256]{2,1,0:T(8,128)(2,1)S(1)}, bf16[4,384,256]{2,1,0:T(8,128)(2,1)S(1)}) custom-call(f32[8,256,128]{2,1,0:T(8,128)S(1)} %get-tuple-element.22.pos_ref, bf16[4,4,256,256]{3,2,1,0:T(8,128)(2,1)S(1)} %get-tuple-element.23.own_ref, bf16[4,4,256,256]{3,2,1,0:T(8,128)(2,1)S(1)} %collective-permute-done.other_ref, ...), custom_call_target="tpu_custom_call" | custom-call | flops 5000000000 | bytes 1048576 | tf_op jit(solution)/shard_map/attention_outer/pallas_call | solution.py:153
  9.5 3.4 %collective-permute-start.3 = (bf16[4,384,256]{2,1,0:T(8,128)(2,1)S(1)}, bf16[4,384,256]{2,1,0:T(8,128)(2,1)S(1)}, u32[]{:S(2)}, u32[]{:S(2)}) collective-permute-start(bf16[4,384,256]{2,1,0:T(8,128)(2,1)S(1)} %get-tuple-element.31.m3_ref.near_ref), channel_id=1, source_target_pairs={{0,1},{1,2},{2,3},{3,4},{4,5},{5,6},{6,7},{7,8},{8,9},{9,10},{10,1... | collective-permute-start | bytes 2359304 | tf_op jit(solution)/shard_map/ppermute | solution.py:314
  12.9 0.0 copy-start
  13.0 2.6 %collective-permute-start.2 = (bf16[4,384,256]{2,1,0:T(8,128)(2,1)S(1)}, bf16[4,384,256]{2,1,0:T(8,128)(2,1)S(1)}, u32[]{:S(2)}, u32[]{:S(2)}) collective-permute-start(bf16[4,384,256]{2,1,0:T(8,128)(2,1)S(1)} %get-tuple-element.29.before_ref.m0_ref.near_ref), channel_id=1, source_target_pairs={{1,0},{2,1},{3,2},{4,3},{5,4},{6,5},{7,6},{8,7},{9,8},{10,9},{11,1... | collective-permute-start | bytes 2359304 | tf_op jit(solution)/shard_map/ppermute | solution.py:315
  15.5 6.0 %attention_inner.1 = (bf16[4,256,256]{2,1,0:T(8,128)(2,1)S(1)}, bf16[4,256,256]{2,1,0:T(8,128)(2,1)S(1)}) custom-call(f32[8,256,128]{2,1,0:T(8,128)S(1)} %get-tuple-element.22.pos_ref, bf16[4,4,256,256]{3,2,1,0:T(8,128)(2,1)S(1)} %get-tuple-element.23.own_ref, bf16[4,4,256,256]{3,2,1,0:T(8,128)(2,1)S(1)} %collective-permute-done.other_ref, ...), custom_call_target="tpu_custom_call" | custom-call | flops 7000000000 | bytes 1048576 | tf_op jit(solution)/shard_map/attention_inner/pallas_call | solution.py:153
  21.6 2.7 %collective-permute-start.1 = (bf16[4,256,256]{2,1,0:T(8,128)(2,1)S(1)}, bf16[4,256,256]{2,1,0:T(8,128)(2,1)S(1)}, u32[]{:S(2)}, u32[]{:S(2)}) collective-permute-start(bf16[4,256,256]{2,1,0:T(8,128)(2,1)S(1)} %get-tuple-element.30.m1_ref.far_ref), channel_id=1, source_target_pairs={{1,0},{2,1},{3,2},{4,3},{5,4},{6,5},{7,6},{8,7},{9,8},{10,9},{11,1... | collective-permute-start | bytes 1572872 | tf_op jit(solution)/shard_map/ppermute | solution.py:319
  24.3 0.0 copy-start.1
  24.3 0.0 copy-start.3
  24.4 7.6 %collective-permute-start.4 = (bf16[4,256,256]{2,1,0:T(8,128)(2,1)S(1)}, bf16[4,256,256]{2,1,0:T(8,128)(2,1)S(1)}, u32[]{:S(2)}, u32[]{:S(2)}) collective-permute-start(bf16[4,256,256]{2,1,0:T(8,128)(2,1)S(1)} %get-tuple-element.32.m2_ref.far_ref), channel_id=1, source_target_pairs={{0,1},{1,2},{2,3},{3,4},{4,5},{5,6},{6,7},{7,8},{8,9},{9,10},{10,1... | collective-permute-start | bytes 1572872 | tf_op jit(solution)/shard_map/ppermute | solution.py:318
  32.0 0.0 copy-done
  32.0 3.1 %stage_one.1.mid_ref = bf16[4,2,256,256]{3,2,1,0:T(8,128)(2,1)S(1)} custom-call(bf16[4,384,256]{2,1,0:T(8,128)(2,1)S(1)} %get-tuple-element.29.before_ref.m0_ref.near_ref, bf16[4,256,256]{2,1,0:T(8,128)(2,1)S(1)} %get-tuple-element.30.m1_ref.far_ref, bf16[4,256,256]{2,1,0:T(8,128)(2,1)S(1)} %get-tuple-element.32.m2_ref.far_ref, ...), custom_call_target="tpu_custom_call" | custom-call | flops 3000000000 | bytes 1048576 | tf_op jit(solution)/shard_map/stage_one/pallas_call | solution.py:153
  35.2 0.0 collective-permute-done.3.halo_ref
  35.2 0.0 copy-done.1
  35.2 0.0 copy-done.3
  35.2 6.2 %stage_two_0.1 = (bf16[4,256,256]{2,1,0:T(8,128)(2,1)S(1)}, f32[4,256,256]{2,1,0:T(8,128)S(1)}, f32[4,256,256]{2,1,0:T(8,128)S(1)}) custom-call(bf16[4,384,256]{2,1,0:T(8,128)(2,1)S(1)} %collective-permute-done.3.halo_ref, bf16[4,384,256]{2,1,0:T(8,128)(2,1)S(1)} %get-tuple-element.29.before_ref.m0_ref.near_ref, ...), custom_call_target="tpu_custom_call" | custom-call | flops 5000000000 | bytes 1048576 | tf_op jit(solution)/shard_map/stage_two_0/pallas_call | solution.py:153
  41.4 0.0 collective-permute-done.2.halo_ref
  41.5 5.1 %stage_two_1.1 = (bf16[4,256,256]{2,1,0:T(8,128)(2,1)S(1)}, f32[4,256,256]{2,1,0:T(8,128)S(1)}, f32[4,256,256]{2,1,0:T(8,128)S(1)}) custom-call(bf16[4,384,256]{2,1,0:T(8,128)(2,1)S(1)} %collective-permute-done.2.halo_ref, bf16[4,384,256]{2,1,0:T(8,128)(2,1)S(1)} %get-tuple-element.31.m3_ref.near_ref, ...), custom_call_target="tpu_custom_call" | custom-call | flops 5000000000 | bytes 1048576 | tf_op jit(solution)/shard_map/stage_two_1/pallas_call | solution.py:153
  46.5 0.0 collective-permute-done.4.halo_ref
  46.5 2.0 %stage_three_0.1.rest_1_ = bf16[4,4,256,256]{3,2,1,0:T(8,128)(2,1)} custom-call(bf16[4,256,256]{2,1,0:T(8,128)(2,1)S(1)} %collective-permute-done.4.halo_ref, bf16[4,256,256]{2,1,0:T(8,128)(2,1)S(1)} %get-tuple-element.36.inner_ref.rest_0_, f32[4,256,256]{2,1,0:T(8,128)S(1)} %get-tuple-element.37.first_ref, f32[4,256,256]{2,1,0:T(8,128)S(1)} %get-tuple-element.38.second_ref, ...), custom_call_target="tpu_custom_call" | custom-call | flops 2000000000 | bytes 1048576 | tf_op jit(solution)/shard_map/stage_three_0/pallas_call | solution.py:280
  48.6 1.2 %collective-permute-done.1.halo_ref = bf16[4,256,256]{2,1,0:T(8,128)(2,1)S(1)} collective-permute-done((bf16[4,256,256]{2,1,0:T(8,128)(2,1)S(1)}, bf16[4,256,256]{2,1,0:T(8,128)(2,1)S(1)}, u32[]{:S(2)}, u32[]{:S(2)}) %collective-permute-start.1) | collective-permute-done | bytes 524320 | tf_op jit(solution)/shard_map/ppermute | solution.py:319
  49.7 2.0 %stage_three_1.1 = bf16[4,4,256,256]{3,2,1,0:T(8,128)(2,1)} custom-call(bf16[4,256,256]{2,1,0:T(8,128)(2,1)S(1)} %collective-permute-done.1.halo_ref, bf16[4,256,256]{2,1,0:T(8,128)(2,1)S(1)} %get-tuple-element.33.rest_0_.inner_ref, f32[4,256,256]{2,1,0:T(8,128)S(1)} %get-tuple-element.34.first_ref, ...), custom_call_target="tpu_custom_call", output_to_operand_aliasing={{}: (7, {})} | custom-call | flops 2000000000 | bytes 1048576 | tf_op jit(solution)/shard_map/stage_three_1/pallas_call | solution.py:280
Async XLA Ops:
  0.0 4.4 %copy-start.2 = (bf16[4,2,128,256]{3,2,1,0:T(8,128)(2,1)S(1)}, bf16[4,2,128,256]{3,2,1,0:T(8,128)(2,1)}, u32[]{:S(2)}) copy-start(bf16[4,2,128,256]{3,2,1,0:T(8,128)(2,1)} %coarse_ref.5) | copy-start | bytes 1572868
  0.0 4.4 %collective-permute-start = (bf16[4,4,256,256]{3,2,1,0:T(8,128)(2,1)}, bf16[4,4,256,256]{3,2,1,0:T(8,128)(2,1)S(1)}, u32[]{:S(2)}, u32[]{:S(2)}) collective-permute-start(bf16[4,4,256,256]{3,2,1,0:T(8,128)(2,1)} %own_hbm.1), channel_id=1, source_target_pairs={{0,64},{64,0},{1,65},{65,1},{2,66},{66,2},{3,67},{67,3},{4,68},{68... | collective-permute-start | bytes 6291464 | tf_op jit(solution)/shard_map/ppermute | solution.py:308
  9.5 25.6 %collective-permute-start.3 = (bf16[4,384,256]{2,1,0:T(8,128)(2,1)S(1)}, bf16[4,384,256]{2,1,0:T(8,128)(2,1)S(1)}, u32[]{:S(2)}, u32[]{:S(2)}) collective-permute-start(bf16[4,384,256]{2,1,0:T(8,128)(2,1)S(1)} %get-tuple-element.31.m3_ref.near_ref), channel_id=1, source_target_pairs={{0,1},{1,2},{2,3},{3,4},{4,5},{5,6},{6,7},{7,8},{8,9},{9,10},{10,1... | collective-permute-start | bytes 2359304 | tf_op jit(solution)/shard_map/ppermute | solution.py:314
  12.9 19.1 %copy-start = (bf16[3,3,256,256]{3,2,1,0:T(8,128)(2,1)S(1)}, bf16[3,3,256,256]{3,2,1,0:T(8,128)(2,1)}, u32[]{:S(2)}) copy-start(bf16[3,3,256,256]{3,2,1,0:T(8,128)(2,1)} %w1_ref.9) | copy-start | bytes 3538948
  13.0 28.5 %collective-permute-start.2 = (bf16[4,384,256]{2,1,0:T(8,128)(2,1)S(1)}, bf16[4,384,256]{2,1,0:T(8,128)(2,1)S(1)}, u32[]{:S(2)}, u32[]{:S(2)}) collective-permute-start(bf16[4,384,256]{2,1,0:T(8,128)(2,1)S(1)} %get-tuple-element.29.before_ref.m0_ref.near_ref), channel_id=1, source_target_pairs={{1,0},{2,1},{3,2},{4,3},{5,4},{6,5},{7,6},{8,7},{9,8},{10,9},{11,1... | collective-permute-start | bytes 2359304 | tf_op jit(solution)/shard_map/ppermute | solution.py:315
  21.6 28.2 %collective-permute-start.1 = (bf16[4,256,256]{2,1,0:T(8,128)(2,1)S(1)}, bf16[4,256,256]{2,1,0:T(8,128)(2,1)S(1)}, u32[]{:S(2)}, u32[]{:S(2)}) collective-permute-start(bf16[4,256,256]{2,1,0:T(8,128)(2,1)S(1)} %get-tuple-element.30.m1_ref.far_ref), channel_id=1, source_target_pairs={{1,0},{2,1},{3,2},{4,3},{5,4},{6,5},{7,6},{8,7},{9,8},{10,9},{11,1... | collective-permute-start | bytes 1572872 | tf_op jit(solution)/shard_map/ppermute | solution.py:319
  24.3 10.8 %copy-start.1 = (bf16[3,3,256,256]{3,2,1,0:T(8,128)(2,1)S(1)}, bf16[3,3,256,256]{3,2,1,0:T(8,128)(2,1)}, u32[]{:S(2)}) copy-start(bf16[3,3,256,256]{3,2,1,0:T(8,128)(2,1)} %w2_ref.7) | copy-start | bytes 3538948
  24.3 10.8 %copy-start.3 = (bf16[2,256,256]{2,1,0:T(8,128)(2,1)S(1)}, bf16[2,256,256]{2,1,0:T(8,128)(2,1)}, u32[]{:S(2)}) copy-start(bf16[2,256,256]{2,1,0:T(8,128)(2,1)} %constant.5.clone.lift_ref) | copy-start | bytes 786436
  24.4 22.2 %collective-permute-start.4 = (bf16[4,256,256]{2,1,0:T(8,128)(2,1)S(1)}, bf16[4,256,256]{2,1,0:T(8,128)(2,1)S(1)}, u32[]{:S(2)}, u32[]{:S(2)}) collective-permute-start(bf16[4,256,256]{2,1,0:T(8,128)(2,1)S(1)} %get-tuple-element.32.m2_ref.far_ref), channel_id=1, source_target_pairs={{0,1},{1,2},{2,3},{3,4},{4,5},{5,6},{6,7},{7,8},{8,9},{9,10},{10,1... | collective-permute-start | bytes 1572872 | tf_op jit(solution)/shard_map/ppermute | solution.py:318

commit v3 on v2

--- a/solution.py
+++ b/solution.py
@@ -43,37 +43,52 @@
     frames = own_ref.shape[0]
     base = lax.axis_index("tm") * frames
     for f in range(frames):
-        normed_row(own_ref, f, row, pos_ref[base + f], norm_s.at[f])
-        y = dot(wqkv_ref[...], norm_s[f])
+        norm = norm_s.at[at_row * frames + f]
+        normed_row(own_ref, f, row, pos_ref[base + f], norm)
+        y = dot(wqkv_ref[...], norm[...])
         q_ref[at_row, f] = y[:C]
         k_ref[at_row, f] = y[C:2 * C]
         v_ref[at_row, f] = y[2 * C:]
 
 
-def attention_row(at_row, row, pos_ref, own_ref, other_ref, wkv_ref, wo_ref, q_ref, ko_ref, vo_ref, out_ref,
-                  norm_s, k_s, v_s, att_s):
-    frames = own_ref.shape[0]
+def other_row(n, row, pos_ref, other_ref, wqkv_ref, norm_s, k_s, v_s):
+    frames = other_ref.shape[0]
+    base = (1 - lax.axis_index("tm")) * frames
+    for f in range(frames):
+        norm = norm_s.at[n * frames + f]
+        normed_row(other_ref, f, row, pos_ref[base + f], norm)
+        y = dot(wqkv_ref[C:], norm[...])
+        k_s[n, f] = y[:C]
+        v_s[n, f] = y[C:]
+
+
+def scores(n, lanes, q_ref, key_refs):
+    frames = q_ref.shape[1]
+
+    def step(d, acc):
+        at = pl.ds(pl.multiple_of(d * HEADS, HEADS), HEADS)
+        qs = [q_ref[n, a, at, lanes] for a in range(frames)]
+        ks = [ref[n, b, at, lanes] for ref in key_refs for b in range(frames)]
+        return tuple(total + q * k for total, (q, k) in zip(acc, [(q, k) for q in qs for k in ks]))
+
+    zero = jnp.zeros((HEADS, 128), F32)
+    return lax.fori_loop(0, D, step, (zero,) * (frames * frames * len(key_refs)), unroll=16 // len(key_refs))
+
+
+def attend_row(n, q_ref, ko_ref, vo_ref, k_s, v_s, att_s, prior_ref=None):
+    frames = q_ref.shape[1]
     keys = 2 * frames
-    base = (1 - lax.axis_index("tm")) * frames
-
-    for f in range(frames):
-        normed_row(other_ref, f, row, pos_ref[base + f], norm_s.at[f])
-        y = dot(wkv_ref[C:], norm_s[f])
-        k_s[f] = y[:C]
-        v_s[f] = y[C:]
-
     factor = float(np.log2(np.e) / np.sqrt(D))
     for half in range(W // 128):
         lanes = slice(half * 128, half * 128 + 128)
-
-        def score(d, acc):
-            at = pl.ds(pl.multiple_of(d * HEADS, HEADS), HEADS)
-            qs = [q_ref[at_row, a, at, lanes] for a in range(frames)]
-            ks = [ko_ref[at_row, b, at, lanes] for b in range(frames)] + [k_s[b, at, lanes] for b in range(frames)]
-            return tuple(acc[a * keys + b] + qs[a] * ks[b] for a in range(frames) for b in range(keys))
-
-        zero = jnp.zeros((HEADS, 128), F32)
-        acc = lax.fori_loop(0, D, score, (zero,) * (frames * keys), unroll=4)
+        if prior_ref is None:
+            acc = scores(n, lanes, q_ref, (ko_ref, k_s))
+        else:
+            late = scores(n, lanes, q_ref, (k_s,))
+            acc = []
+            for a in range(frames):
+                acc += [prior_ref[n, half, a * frames + b] for b in range(frames)]
+                acc += late[a * frames:(a + 1) * frames]
         weights = []
         for a in range(frames):
             line = acc[a * keys:(a + 1) * keys]
@@ -91,7 +106,7 @@
             outs = [[] for _ in range(frames)]
             for sub in range(2):
                 at = pl.ds(pl.multiple_of(d2 * 2 * HEADS + sub * HEADS, HEADS), HEADS)
-                vs = [vo_ref[at_row, b, at, lanes] for b in range(frames)] + [v_s[b, at, lanes] for b in range(frames)]
+                vs = [vo_ref[n, b, at, lanes] for b in range(frames)] + [v_s[n, b, at, lanes] for b in range(frames)]
                 for a in range(frames):
                     total = weights[a * keys] * vs[0]
                     for b in range(1, keys):
@@ -99,18 +114,20 @@
                     outs[a].append(total)
             at = pl.ds(pl.multiple_of(d2 * 2 * HEADS, 2 * HEADS), 2 * HEADS)
             for a in range(frames):
-                att_s[a, at, lanes] = jnp.concatenate(outs[a], axis=0).astype(BF16)
+                att_s[n, a, at, lanes] = jnp.concatenate(outs[a], axis=0).astype(BF16)
             return 0
 
-        lax.fori_loop(0, D // 2, gather, 0, unroll=2)
-
-    for a in range(frames):
-        branch = lax.dot_general(att_s[a], wo_ref[...], (((0,), (0,)), ((), ())), preferred_element_type=F32)
+        lax.fori_loop(0, D // 2, gather, 0, unroll=4)
+
+
+def out_row(n, row, own_ref, wo_ref, att_s, out_ref):
+    for a in range(own_ref.shape[0]):
+        branch = lax.dot_general(att_s[n, a], wo_ref[...], (((0,), (0,)), ((), ())), preferred_element_type=F32)
         out_ref[a, :W] = (own_ref[a, row].astype(F32) + branch).astype(BF16)
 
 
 def own_body(pos_hbm, own_hbm, wq_hbm, wk_hbm, wv_hbm, wo_hbm,
-             pos_ref, own_ref, wqkv_ref, wor_ref, q_ref, k_ref, v_ref, w_s, norm_s, sems):
+             pos_ref, own_ref, wqkv_ref, wor_ref, q_ref, k_ref, v_ref, prior_ref, w_s, norm_s, sems):
     frames, rows = own_hbm.shape[:2]
     loads = [pltpu.make_async_copy(ref, w_s.at[n], sems.at[n]) for n, ref in enumerate((wq_hbm, wk_hbm, wv_hbm, wo_hbm))]
     loads.append(pltpu.make_async_copy(pos_hbm, pos_ref, sems.at[4]))
@@ -130,23 +147,36 @@
         load.wait()
     for n, row in enumerate((0, own_ref.shape[1] - 1)):
         own_row(n, row, pos_ref, own_ref, wqkv_ref, q_ref, k_ref, v_ref, norm_s)
-
-
-def outer_body(pos_ref, own_ref, other_ref, wqkv_ref, wo_ref, q_ref, k_ref, v_ref, coarse_ref, down_ref, up_ref,
-               norm_s, k_s, v_s, att_s):
-    for n, (row, ref) in enumerate(((0, down_ref), (own_ref.shape[1] - 1, up_ref))):
-        attention_row(n, row, pos_ref, own_ref, other_ref, wqkv_ref, wo_ref, q_ref, k_ref, v_ref, ref,
-                      norm_s, k_s, v_s, att_s)
+    for n in range(2):
+        for half in range(W // 128):
+            lanes = slice(half * 128, half * 128 + 128)
+            for i, total in enumerate(scores(n, lanes, q_ref, (k_ref,))):
+                prior_ref[n, half, i] = total
+
+
+def outer_body(pos_ref, own_ref, other_ref, wqkv_ref, wo_ref, q_ref, k_ref, v_ref, prior_ref, coarse_ref,
+               down_ref, up_ref, norm_s, k_s, v_s, att_s):
+    rows = (0, own_ref.shape[1] - 1)
+    for n, row in enumerate(rows):
+        other_row(n, row, pos_ref, other_ref, wqkv_ref, norm_s, k_s, v_s)
+    for n in range(2):
+        attend_row(n, q_ref, k_ref, v_ref, k_s, v_s, att_s, prior_ref)
+    for n, (row, ref) in enumerate(zip(rows, (down_ref, up_ref))):
+        out_row(n, row, own_ref, wo_ref, att_s, ref)
         ref[:, W:] = coarse_ref[:, n * (coarse_ref.shape[1] - 1)]
 
 
 def inner_body(pos_ref, own_ref, other_ref, wqkv_ref, wo_ref, before_ref, down_ref, up_ref,
-               norm_s, k_s, v_s, att_s, q_s, ko_s, vo_s):
+               norm_s, k_s, v_s, att_s, q_s, ko_s, vo_s, normo_s):
     del before_ref
-    for row, ref in ((1, down_ref), (own_ref.shape[1] - 2, up_ref)):
-        own_row(0, row, pos_ref, own_ref, wqkv_ref, q_s, ko_s, vo_s, norm_s)
-        attention_row(0, row, pos_ref, own_ref, other_ref, wqkv_ref, wo_ref, q_s, ko_s, vo_s, ref,
-                      norm_s, k_s, v_s, att_s)
+    rows = (1, own_ref.shape[1] - 2)
+    for n, row in enumerate(rows):
+        own_row(n, row, pos_ref, own_ref, wqkv_ref, q_s, ko_s, vo_s, normo_s)
+        other_row(n, row, pos_ref, other_ref, wqkv_ref, norm_s, k_s, v_s)
+    for n in range(2):
+        attend_row(n, q_s, ko_s, vo_s, k_s, v_s, att_s)
+    for n, (row, ref) in enumerate(zip(rows, (down_ref, up_ref))):
+        out_row(n, row, own_ref, wo_ref, att_s, ref)
 
 
 def call(body, name, args, outs, scratch, micros, space=pltpu.VMEM):
@@ -167,15 +197,16 @@
     wide = ((2, frames, C, W), F32)
     args = [pltpu.with_memory_space_constraint(a, pltpu.HBM) for a in (pos, own, *weights)]
     return call(own_body, "own_projections", args,
-                [(pos.shape, F32), (own.shape, BF16), ((3 * C, C), BF16), ((C, C), BF16), wide, wide, wide],
-                [pltpu.VMEM((4, C, C), BF16), pltpu.VMEM((frames, C, W), BF16), pltpu.SemaphoreType.DMA((6,))], 6, pltpu.HBM)
+                [(pos.shape, F32), (own.shape, BF16), ((3 * C, C), BF16), ((C, C), BF16), wide, wide, wide,
+                 ((2, W // 128, frames * frames, HEADS, 128), F32)],
+                [pltpu.VMEM((4, C, C), BF16), pltpu.VMEM((2 * frames, C, W), BF16), pltpu.SemaphoreType.DMA((6,))], 6, pltpu.HBM)
 
 
 def attention(body, name, args, width, extra, micros):
     frames = args[1].shape[0]
     return call(body, name, args, [((frames, width, C), BF16)] * 2,
-                [pltpu.VMEM((frames, C, W), BF16), pltpu.VMEM((frames, C, W), F32),
-                 pltpu.VMEM((frames, C, W), F32), pltpu.VMEM((frames, C, W), BF16)] + extra, micros)
+                [pltpu.VMEM((2 * frames, C, W), BF16), pltpu.VMEM((2, frames, C, W), F32),
+                 pltpu.VMEM((2, frames, C, W), F32), pltpu.VMEM((2, frames, C, W), BF16)] + extra, micros)
 
 
 def clear_pads(pad_s):
@@ -308,13 +339,14 @@
     other = lax.ppermute(fine, "tm", [(0, 1), (1, 0)])
     pos = jnp.asarray(encode_table(2 * frames, C))
     ready = own_projections(pos, fine, w_query, w_key, w_value, w_out)
-    held_pos, held, wqkv, wo, q, k, v = ready
-    m0, m3 = attention(outer_body, "attention_outer", (held_pos, held, other, wqkv, wo, q, k, v, coarse), W + HALF,
+    held_pos, held, wqkv, wo, *early = ready
+    m0, m3 = attention(outer_body, "attention_outer", (held_pos, held, other, wqkv, wo, *early, coarse), W + HALF,
                        [], 5)
     above = lax.ppermute(m3, "space", up)
     below = lax.ppermute(m0, "space", down)
-    wide = pltpu.VMEM((1, frames, C, W), F32)
-    m1, m2 = attention(inner_body, "attention_inner", (held_pos, held, other, wqkv, wo, m0), W, [wide] * 3, 7)
+    wide = pltpu.VMEM((2, frames, C, W), F32)
+    m1, m2 = attention(inner_body, "attention_inner", (held_pos, held, other, wqkv, wo, m0), W,
+                       [wide] * 3 + [pltpu.VMEM((2 * frames, C, W), BF16)], 7)
     above2 = lax.ppermute(m2, "space", up)
     below2 = lax.ppermute(m1, "space", down)
     (mid,) = call(stage_one, "stage_one", (m0, m1, m2, m3, conv_first), [((frames, 2, W, C), BF16)],

time: 52.4 us -> 50.9 us (0.971)
  Pallas kernels: 33.3 us -> 31.7 us
    pallas_call x6, Pallas kernels: 29.2 us -> 27.6 us  [call(): pl.pallas_call(body, in_specs=[pl.BlockSpec(memory_space=space)] * len(ar...]
    ppermute x1, waiting for transfers between devices: 1.18 us -> 2.11 us  [local(): below2 = lax.ppermute(m1, 'space', down)]
    ppermute x1, waiting for transfers between devices: 0.77 us -> 0.17 us  [local(): other = lax.ppermute(fine, 'tm', [(0, 1), (1, 0)])]
  transfers between devices with their start and end apart: 5 -> 5, of which waited for: 2 -> 2; matrix products, arithmetic and copies ran while one was open for 0% -> 0% of each run, Pallas kernels for 50% -> 51%
where the time goes in v3:
time: 50.9 us; the launch traced here: 50.7 us
  Pallas kernels  31.7 us (62%)
  starting transfers between devices  16.4 us (32%)
  waiting for transfers between devices  2.3 us (5%)
    pallas_call x6, Pallas kernels, call(): pl.pallas_call(body, in_specs=[pl.BlockSpec(memory_space=space)] * len(ar...  27.6 us
    ppermute x1, starting transfers between devices, local(): above2 = lax.ppermute(m2, 'space', up)  7.64 us
    pallas_call x2, Pallas kernels, last_stage(): pl.pallas_call(functools.partial(stage_three, side), in_specs=[pl.BlockSp...  4.06 us
    ppermute x1, starting transfers between devices, local(): above = lax.ppermute(m3, 'space', up)  3.4 us
    ppermute x1, starting transfers between devices, local(): below2 = lax.ppermute(m1, 'space', down)  2.74 us
    ppermute x1, starting transfers between devices, local(): below = lax.ppermute(m0, 'space', down)  2.58 us
    ppermute x1, waiting for transfers between devices, local(): below2 = lax.ppermute(m1, 'space', down)  2.11 us
  transfers between devices with their start and end apart: 5, of which 2 were waited for; matrix products, arithmetic and copies ran while one was open for 0% of the time, Pallas kernels for 51%

profile of v3, /device:TPU:30, one launch (start us, length us, event | category | flops | bytes accessed | tf_op | source)
XLA Modules:
  0.0 50.7 jit_solution(16216642008209640846)
XLA Ops:
  0.0 0.0 copy-start.2
  0.0 0.0 collective-permute-start
  0.0 4.2 %own_projections.1 = (f32[8,256,128]{2,1,0:T(8,128)S(1)}, bf16[4,4,256,256]{3,2,1,0:T(8,128)(2,1)S(1)}, bf16[768,256]{1,0:T(8,128)(2,1)S(1)}, bf16[256,256]{1,0:...) custom-call(f32[8,256,128]{2,1,0:T(8,128)} %constant.4.clone.pos_hbm, ...), custom_call_target="tpu_custom_call" | custom-call | flops 6000000000 | bytes 1048576 | tf_op jit(solution)/shard_map/own_projections/pallas_call | solution.py:183
  4.2 0.2 collective-permute-done.other_ref
  4.4 0.0 copy-done.2
  4.4 3.7 %attention_outer.1 = (bf16[4,384,256]{2,1,0:T(8,128)(2,1)S(1)}, bf16[4,384,256]{2,1,0:T(8,128)(2,1)S(1)}) custom-call(f32[8,256,128]{2,1,0:T(8,128)S(1)} %get-tuple-element.23.pos_ref, bf16[4,4,256,256]{3,2,1,0:T(8,128)(2,1)S(1)} %get-tuple-element.24.own_ref, bf16[4,4,256,256]{3,2,1,0:T(8,128)(2,1)S(1)} %collective-permute-done.other_ref, ...), custom_call_target="tpu_custom_call" | custom-call | flops 5000000000 | bytes 1048576 | tf_op jit(solution)/shard_map/attention_outer/pallas_call | solution.py:183
  8.1 3.4 %collective-permute-start.3 = (bf16[4,384,256]{2,1,0:T(8,128)(2,1)S(1)}, bf16[4,384,256]{2,1,0:T(8,128)(2,1)S(1)}, u32[]{:S(2)}, u32[]{:S(2)}) collective-permute-start(bf16[4,384,256]{2,1,0:T(8,128)(2,1)S(1)} %get-tuple-element.33.m3_ref.near_ref), channel_id=1, source_target_pairs={{0,1},{1,2},{2,3},{3,4},{4,5},{5,6},{6,7},{7,8},{8,9},{9,10},{10,1... | collective-permute-start | bytes 2359304 | tf_op jit(solution)/shard_map/ppermute | solution.py:345
  11.5 0.0 copy-start
  11.5 2.6 %collective-permute-start.2 = (bf16[4,384,256]{2,1,0:T(8,128)(2,1)S(1)}, bf16[4,384,256]{2,1,0:T(8,128)(2,1)S(1)}, u32[]{:S(2)}, u32[]{:S(2)}) collective-permute-start(bf16[4,384,256]{2,1,0:T(8,128)(2,1)S(1)} %get-tuple-element.31.before_ref.m0_ref.near_ref), channel_id=1, source_target_pairs={{1,0},{2,1},{3,2},{4,3},{5,4},{6,5},{7,6},{8,7},{9,8},{10,9},{11,1... | collective-permute-start | bytes 2359304 | tf_op jit(solution)/shard_map/ppermute | solution.py:346
  14.1 5.3 %attention_inner.1 = (bf16[4,256,256]{2,1,0:T(8,128)(2,1)S(1)}, bf16[4,256,256]{2,1,0:T(8,128)(2,1)S(1)}) custom-call(f32[8,256,128]{2,1,0:T(8,128)S(1)} %get-tuple-element.23.pos_ref, bf16[4,4,256,256]{3,2,1,0:T(8,128)(2,1)S(1)} %get-tuple-element.24.own_ref, bf16[4,4,256,256]{3,2,1,0:T(8,128)(2,1)S(1)} %collective-permute-done.other_ref, ...), custom_call_target="tpu_custom_call" | custom-call | flops 7000000000 | bytes 1048576 | tf_op jit(solution)/shard_map/attention_inner/pallas_call | solution.py:183
  19.4 2.7 %collective-permute-start.1 = (bf16[4,256,256]{2,1,0:T(8,128)(2,1)S(1)}, bf16[4,256,256]{2,1,0:T(8,128)(2,1)S(1)}, u32[]{:S(2)}, u32[]{:S(2)}) collective-permute-start(bf16[4,256,256]{2,1,0:T(8,128)(2,1)S(1)} %get-tuple-element.32.m1_ref.far_ref), channel_id=1, source_target_pairs={{1,0},{2,1},{3,2},{4,3},{5,4},{6,5},{7,6},{8,7},{9,8},{10,9},{11,1... | collective-permute-start | bytes 1572872 | tf_op jit(solution)/shard_map/ppermute | solution.py:351
  22.1 0.0 copy-start.1
  22.2 0.0 copy-start.3
  22.2 7.6 %collective-permute-start.4 = (bf16[4,256,256]{2,1,0:T(8,128)(2,1)S(1)}, bf16[4,256,256]{2,1,0:T(8,128)(2,1)S(1)}, u32[]{:S(2)}, u32[]{:S(2)}) collective-permute-start(bf16[4,256,256]{2,1,0:T(8,128)(2,1)S(1)} %get-tuple-element.34.m2_ref.far_ref), channel_id=1, source_target_pairs={{0,1},{1,2},{2,3},{3,4},{4,5},{5,6},{6,7},{7,8},{8,9},{9,10},{10,1... | collective-permute-start | bytes 1572872 | tf_op jit(solution)/shard_map/ppermute | solution.py:350
  29.8 0.0 copy-done
  29.8 3.1 %stage_one.1.mid_ref = bf16[4,2,256,256]{3,2,1,0:T(8,128)(2,1)S(1)} custom-call(bf16[4,384,256]{2,1,0:T(8,128)(2,1)S(1)} %get-tuple-element.31.before_ref.m0_ref.near_ref, bf16[4,256,256]{2,1,0:T(8,128)(2,1)S(1)} %get-tuple-element.32.m1_ref.far_ref, bf16[4,256,256]{2,1,0:T(8,128)(2,1)S(1)} %get-tuple-element.34.m2_ref.far_ref, ...), custom_call_target="tpu_custom_call" | custom-call | flops 3000000000 | bytes 1048576 | tf_op jit(solution)/shard_map/stage_one/pallas_call | solution.py:183
  33.0 0.0 collective-permute-done.3.halo_ref
  33.0 0.0 copy-done.1
  33.0 0.0 copy-done.3
  33.0 6.2 %stage_two_0.1 = (bf16[4,256,256]{2,1,0:T(8,128)(2,1)S(1)}, f32[4,256,256]{2,1,0:T(8,128)S(1)}, f32[4,256,256]{2,1,0:T(8,128)S(1)}) custom-call(bf16[4,384,256]{2,1,0:T(8,128)(2,1)S(1)} %collective-permute-done.3.halo_ref, bf16[4,384,256]{2,1,0:T(8,128)(2,1)S(1)} %get-tuple-element.31.before_ref.m0_ref.near_ref, ...), custom_call_target="tpu_custom_call" | custom-call | flops 5000000000 | bytes 1048576 | tf_op jit(solution)/shard_map/stage_two_0/pallas_call | solution.py:183
  39.3 0.0 collective-permute-done.2.halo_ref
  39.3 5.1 %stage_two_1.1 = (bf16[4,256,256]{2,1,0:T(8,128)(2,1)S(1)}, f32[4,256,256]{2,1,0:T(8,128)S(1)}, f32[4,256,256]{2,1,0:T(8,128)S(1)}) custom-call(bf16[4,384,256]{2,1,0:T(8,128)(2,1)S(1)} %collective-permute-done.2.halo_ref, bf16[4,384,256]{2,1,0:T(8,128)(2,1)S(1)} %get-tuple-element.33.m3_ref.near_ref, ...), custom_call_target="tpu_custom_call" | custom-call | flops 5000000000 | bytes 1048576 | tf_op jit(solution)/shard_map/stage_two_1/pallas_call | solution.py:183
  44.3 0.0 collective-permute-done.4.halo_ref
  44.3 2.0 %stage_three_0.1.rest_1_ = bf16[4,4,256,256]{3,2,1,0:T(8,128)(2,1)} custom-call(bf16[4,256,256]{2,1,0:T(8,128)(2,1)S(1)} %collective-permute-done.4.halo_ref, bf16[4,256,256]{2,1,0:T(8,128)(2,1)S(1)} %get-tuple-element.38.inner_ref.rest_0_, f32[4,256,256]{2,1,0:T(8,128)S(1)} %get-tuple-element.39.first_ref, f32[4,256,256]{2,1,0:T(8,128)S(1)} %get-tuple-element.40.second_ref, ...), custom_call_target="tpu_custom_call" | custom-call | flops 2000000000 | bytes 1048576 | tf_op jit(solution)/shard_map/stage_three_0/pallas_call | solution.py:311
  46.4 2.1 %collective-permute-done.1.halo_ref = bf16[4,256,256]{2,1,0:T(8,128)(2,1)S(1)} collective-permute-done((bf16[4,256,256]{2,1,0:T(8,128)(2,1)S(1)}, bf16[4,256,256]{2,1,0:T(8,128)(2,1)S(1)}, u32[]{:S(2)}, u32[]{:S(2)}) %collective-permute-start.1) | collective-permute-done | bytes 524320 | tf_op jit(solution)/shard_map/ppermute | solution.py:351
  48.5 2.0 %stage_three_1.1 = bf16[4,4,256,256]{3,2,1,0:T(8,128)(2,1)} custom-call(bf16[4,256,256]{2,1,0:T(8,128)(2,1)S(1)} %collective-permute-done.1.halo_ref, bf16[4,256,256]{2,1,0:T(8,128)(2,1)S(1)} %get-tuple-element.35.rest_0_.inner_ref, f32[4,256,256]{2,1,0:T(8,128)S(1)} %get-tuple-element.36.first_ref, ...), custom_call_target="tpu_custom_call", output_to_operand_aliasing={{}: (7, {})} | custom-call | flops 2000000000 | bytes 1048576 | tf_op jit(solution)/shard_map/stage_three_1/pallas_call | solution.py:311
Async XLA Ops:
  0.0 4.4 %copy-start.2 = (bf16[4,2,128,256]{3,2,1,0:T(8,128)(2,1)S(1)}, bf16[4,2,128,256]{3,2,1,0:T(8,128)(2,1)}, u32[]{:S(2)}) copy-start(bf16[4,2,128,256]{3,2,1,0:T(8,128)(2,1)} %coarse_ref.5) | copy-start | bytes 1572868
  0.0 4.4 %collective-permute-start = (bf16[4,4,256,256]{3,2,1,0:T(8,128)(2,1)}, bf16[4,4,256,256]{3,2,1,0:T(8,128)(2,1)S(1)}, u32[]{:S(2)}, u32[]{:S(2)}) collective-permute-start(bf16[4,4,256,256]{3,2,1,0:T(8,128)(2,1)} %own_hbm.1), channel_id=1, source_target_pairs={{0,64},{64,0},{1,65},{65,1},{2,66},{66,2},{3,67},{67,3},{4,68},{68... | collective-permute-start | bytes 6291464 | tf_op jit(solution)/shard_map/ppermute | solution.py:339
  8.1 24.9 %collective-permute-start.3 = (bf16[4,384,256]{2,1,0:T(8,128)(2,1)S(1)}, bf16[4,384,256]{2,1,0:T(8,128)(2,1)S(1)}, u32[]{:S(2)}, u32[]{:S(2)}) collective-permute-start(bf16[4,384,256]{2,1,0:T(8,128)(2,1)S(1)} %get-tuple-element.33.m3_ref.near_ref), channel_id=1, source_target_pairs={{0,1},{1,2},{2,3},{3,4},{4,5},{5,6},{6,7},{7,8},{8,9},{9,10},{10,1... | collective-permute-start | bytes 2359304 | tf_op jit(solution)/shard_map/ppermute | solution.py:345
  11.5 18.3 %copy-start = (bf16[3,3,256,256]{3,2,1,0:T(8,128)(2,1)S(1)}, bf16[3,3,256,256]{3,2,1,0:T(8,128)(2,1)}, u32[]{:S(2)}) copy-start(bf16[3,3,256,256]{3,2,1,0:T(8,128)(2,1)} %w1_ref.9) | copy-start | bytes 3538948
  11.5 27.7 %collective-permute-start.2 = (bf16[4,384,256]{2,1,0:T(8,128)(2,1)S(1)}, bf16[4,384,256]{2,1,0:T(8,128)(2,1)S(1)}, u32[]{:S(2)}, u32[]{:S(2)}) collective-permute-start(bf16[4,384,256]{2,1,0:T(8,128)(2,1)S(1)} %get-tuple-element.31.before_ref.m0_ref.near_ref), channel_id=1, source_target_pairs={{1,0},{2,1},{3,2},{4,3},{5,4},{6,5},{7,6},{8,7},{9,8},{10,9},{11,1... | collective-permute-start | bytes 2359304 | tf_op jit(solution)/shard_map/ppermute | solution.py:346
  19.4 29.1 %collective-permute-start.1 = (bf16[4,256,256]{2,1,0:T(8,128)(2,1)S(1)}, bf16[4,256,256]{2,1,0:T(8,128)(2,1)S(1)}, u32[]{:S(2)}, u32[]{:S(2)}) collective-permute-start(bf16[4,256,256]{2,1,0:T(8,128)(2,1)S(1)} %get-tuple-element.32.m1_ref.far_ref), channel_id=1, source_target_pairs={{1,0},{2,1},{3,2},{4,3},{5,4},{6,5},{7,6},{8,7},{9,8},{10,9},{11,1... | collective-permute-start | bytes 1572872 | tf_op jit(solution)/shard_map/ppermute | solution.py:351
  22.1 10.8 %copy-start.1 = (bf16[3,3,256,256]{3,2,1,0:T(8,128)(2,1)S(1)}, bf16[3,3,256,256]{3,2,1,0:T(8,128)(2,1)}, u32[]{:S(2)}) copy-start(bf16[3,3,256,256]{3,2,1,0:T(8,128)(2,1)} %w2_ref.7) | copy-start | bytes 3538948
  22.2 10.8 %copy-start.3 = (bf16[2,256,256]{2,1,0:T(8,128)(2,1)S(1)}, bf16[2,256,256]{2,1,0:T(8,128)(2,1)}, u32[]{:S(2)}) copy-start(bf16[2,256,256]{2,1,0:T(8,128)(2,1)} %constant.5.clone.lift_ref) | copy-start | bytes 786436
  22.2 22.2 %collective-permute-start.4 = (bf16[4,256,256]{2,1,0:T(8,128)(2,1)S(1)}, bf16[4,256,256]{2,1,0:T(8,128)(2,1)S(1)}, u32[]{:S(2)}, u32[]{:S(2)}) collective-permute-start(bf16[4,256,256]{2,1,0:T(8,128)(2,1)S(1)} %get-tuple-element.34.m2_ref.far_ref), channel_id=1, source_target_pairs={{0,1},{1,2},{2,3},{3,4},{4,5},{5,6},{6,7},{7,8},{8,9},{9,10},{10,1... | collective-permute-start | bytes 1572872 | tf_op jit(solution)/shard_map/ppermute | solution.py:350

commit v4 on v3

--- a/solution.py
+++ b/solution.py
@@ -24,6 +24,10 @@
     angles = np.arange(frames)[:, None] * inverse[None, :]
     table = np.concatenate([np.sin(angles), np.cos(angles)], axis=1).astype(np.float32)
     return np.ascontiguousarray(np.broadcast_to(table[:, :, None], (frames, width, 128)))
+
+
+def flip():
+    return (lax.axis_index("space") + 1) % 2
 
 
 def dot(a, b):
@@ -145,7 +149,8 @@
     wor_ref[...] = dot(pick, w_s[3]).astype(BF16)
     for load in loads[4:]:
         load.wait()
-    for n, row in enumerate((0, own_ref.shape[1] - 1)):
+    start, last = flip() * (own_ref.shape[1] - 1), own_ref.shape[1] - 1
+    for n, row in enumerate((start, last - start)):
         own_row(n, row, pos_ref, own_ref, wqkv_ref, q_ref, k_ref, v_ref, norm_s)
     for n in range(2):
         for half in range(W // 128):
@@ -154,22 +159,23 @@
                 prior_ref[n, half, i] = total
 
 
-def outer_body(pos_ref, own_ref, other_ref, wqkv_ref, wo_ref, q_ref, k_ref, v_ref, prior_ref, coarse_ref,
+def outer_body(pos_ref, own_ref, other_ref, wqkv_ref, wo_ref, q_ref, k_ref, v_ref, prior_ref,
                down_ref, up_ref, norm_s, k_s, v_s, att_s):
-    rows = (0, own_ref.shape[1] - 1)
+    start, last = flip() * (own_ref.shape[1] - 1), own_ref.shape[1] - 1
+    rows = (start, last - start)
     for n, row in enumerate(rows):
         other_row(n, row, pos_ref, other_ref, wqkv_ref, norm_s, k_s, v_s)
     for n in range(2):
         attend_row(n, q_ref, k_ref, v_ref, k_s, v_s, att_s, prior_ref)
     for n, (row, ref) in enumerate(zip(rows, (down_ref, up_ref))):
         out_row(n, row, own_ref, wo_ref, att_s, ref)
-        ref[:, W:] = coarse_ref[:, n * (coarse_ref.shape[1] - 1)]
-
-
-def inner_body(pos_ref, own_ref, other_ref, wqkv_ref, wo_ref, before_ref, down_ref, up_ref,
+
+
+def inner_body(pos_ref, own_ref, other_ref, wqkv_ref, wo_ref, coarse_ref, before_ref, down_ref, up_ref,
                norm_s, k_s, v_s, att_s, q_s, ko_s, vo_s, normo_s):
     del before_ref
-    rows = (1, own_ref.shape[1] - 2)
+    start = 1 + flip() * (own_ref.shape[1] - 3)
+    rows = (start, own_ref.shape[1] - 1 - start)
     for n, row in enumerate(rows):
         own_row(n, row, pos_ref, own_ref, wqkv_ref, q_s, ko_s, vo_s, normo_s)
         other_row(n, row, pos_ref, other_ref, wqkv_ref, norm_s, k_s, v_s)
@@ -177,6 +183,7 @@
         attend_row(n, q_s, ko_s, vo_s, k_s, v_s, att_s)
     for n, (row, ref) in enumerate(zip(rows, (down_ref, up_ref))):
         out_row(n, row, own_ref, wo_ref, att_s, ref)
+        ref[:, W:] = coarse_ref[:, flip() ^ n]
 
 
 def call(body, name, args, outs, scratch, micros, space=pltpu.VMEM):
@@ -224,9 +231,11 @@
 
 
 def taps(source_s, row, w_ref, total=None, steps=(0, 1, 2)):
+    turned = flip()
     for n, dy in enumerate(steps):
+        tap = dy + turned * (2 - 2 * dy)
         for dx in range(3):
-            part = dot(source_s[dx, (row + n) * W:(row + n + 1) * W], w_ref[dy, dx])
+            part = dot(source_s[dx, (row + n) * W:(row + n + 1) * W], w_ref[tap, dx])
             total = part if total is None else total + part
     return total
 
@@ -258,48 +267,55 @@
     lax.fori_loop(0, m0_ref.shape[0], frame, 0)
 
 
+def at_edge(side):
+    here = lax.axis_index("space")
+    end = (flip() ^ side) * (lax.axis_size("space") - 1)
+    return here == end
+
+
 def stage_two(side, halo_ref, near_ref, far_ref, mid_ref, coarse_ref, lift_ref, w1_ref, w2_ref,
-              inner_ref, first_ref, second_ref, pad_s, in_s, mid_s, coarse_s):
-    edge = lax.axis_index("space") == side * (lax.axis_size("space") - 1)
+              inner_ref, first_ref, second_ref, pad_s, in_s, mid_s):
     steps = (0, 1) if side else (1, 2)
     order = 1 - 2 * side
+    near = flip() ^ side
     clear_pads(pad_s)
 
     def frame(f, _):
-        own = coarse_ref[f, side]
-        coarse_s[side * HALF:(side + 1) * HALF] = jnp.where(edge, own, halo_ref[f, W:])
-        coarse_s[(1 - side) * HALF:(2 - side) * HALF] = own
         for r, ref in enumerate((halo_ref, near_ref, far_ref)[::order]):
             shifted(relu(ref[f, :W]), pad_s.at[r], in_s, r)
         for j in range(2):
             shifted(mid_ref[f, j], pad_s.at[3 + j], mid_s, j + 1 - side)
         shifted(relu(taps(in_s, 0, w1_ref)).astype(BF16), pad_s.at[5], mid_s, 2 * side)
         first_ref[f] = taps(in_s, side, w1_ref, None, steps)
-        total = taps(mid_s, 0, w2_ref, dot(lift_ref[1 - side], coarse_ref[f].reshape(2 * HALF, C)))
+        total = taps(mid_s, 0, w2_ref, dot(lift_ref[1 - near], coarse_ref[f].reshape(2 * HALF, C)))
         inner_ref[f] = (total + far_ref[f, :W].astype(F32)).astype(BF16)
-        total = taps(mid_s, side, w2_ref, dot(lift_ref[side], coarse_s[...]), steps)
-        second_ref[f] = total + near_ref[f, :W].astype(F32)
+        second_ref[f] = taps(mid_s, side, w2_ref, near_ref[f, :W].astype(F32), steps)
         return 0
 
     lax.fori_loop(0, near_ref.shape[0], frame, 0)
 
 
-def stage_three(side, halo_ref, inner_ref, first_ref, second_ref, w1_ref, w2_ref, *rest):
-    out_hbm, pad_s, in_s, mid_s, row_s, sems = rest[-6:]
-    edge = lax.axis_index("space") == side * (lax.axis_size("space") - 1)
+def stage_three(side, halo_ref, coarse_ref, lift_ref, inner_ref, first_ref, second_ref, w1_ref, w2_ref, *rest):
+    out_hbm, pad_s, in_s, mid_s, row_s, coarse_s, sems = rest[-7:]
+    edge = at_edge(side)
+    near = flip() ^ side
     frames = halo_ref.shape[0]
-    copies = [pltpu.make_async_copy(inner_ref.at[f], out_hbm.at[f, 1 + side], sems.at[f]) for f in range(frames)]
-    copies += [pltpu.make_async_copy(row_s.at[f], out_hbm.at[f, 3 * side], sems.at[frames + f]) for f in range(frames)]
+    copies = [pltpu.make_async_copy(inner_ref.at[f], out_hbm.at[f, 1 + near], sems.at[f]) for f in range(frames)]
+    copies += [pltpu.make_async_copy(row_s.at[f], out_hbm.at[f, 3 * near], sems.at[frames + f]) for f in range(frames)]
     for copy in copies[:frames]:
         copy.start()
     clear_pads(pad_s)
     step = (2 * side,)
     for f in range(frames):
-        shifted(relu(halo_ref[f]), pad_s.at[f], in_s, f)
+        shifted(relu(halo_ref[f, :W]), pad_s.at[f], in_s, f)
+        own = coarse_ref[f, near]
+        coarse_s[f, :HALF] = jnp.where(edge, own, halo_ref[f, W:])
+        coarse_s[f, HALF:] = own
         value = relu(taps(in_s, f, w1_ref, first_ref[f], step)).astype(BF16)
         value = jnp.where(edge, jnp.zeros_like(value), value)
         shifted(value, pad_s.at[frames + f], mid_s, f)
-        row_s[f] = taps(mid_s, f, w2_ref, second_ref[f], step).astype(BF16)
+        total = second_ref[f] + dot(lift_ref[0], coarse_s[f])
+        row_s[f] = taps(mid_s, f, w2_ref, total, step).astype(BF16)
         copies[frames + f].start()
     for copy in copies:
         copy.wait()
@@ -315,7 +331,7 @@
         out_specs=pl.BlockSpec(memory_space=pltpu.HBM),
         out_shape=jax.ShapeDtypeStruct((frames, rows, W, C), BF16),
         scratch_shapes=[pads(2 * frames), planes(frames), planes(frames), pltpu.VMEM((frames, W, C), BF16),
-                        pltpu.SemaphoreType.DMA((2 * frames,))],
+                        pltpu.VMEM((frames, 2 * HALF, C), BF16), pltpu.SemaphoreType.DMA((2 * frames,))],
         input_output_aliases={len(args): 0} if before else {},
         compiler_params=pltpu.CompilerParams(vmem_limit_bytes=VMEM_LIMIT),
         cost_estimate=pl.CostEstimate(flops=2 * 10**9, transcendentals=0, bytes_accessed=1 << 20),
@@ -334,21 +350,21 @@
 def local(fine, coarse, w_query, w_key, w_value, w_out, conv_first, conv_second):
     frames = fine.shape[0]
     size = lax.axis_size("space")
-    up = [(i, i + 1) for i in range(size - 1)]
-    down = [(i + 1, i) for i in range(size - 1)]
+    swaps = []
+    for first in (0, 1):
+        pairs = [(i, i + 1) for i in range(first, size - 1, 2)]
+        swaps.append(pairs + [(j, i) for i, j in pairs])
     other = lax.ppermute(fine, "tm", [(0, 1), (1, 0)])
     pos = jnp.asarray(encode_table(2 * frames, C))
     ready = own_projections(pos, fine, w_query, w_key, w_value, w_out)
     held_pos, held, wqkv, wo, *early = ready
-    m0, m3 = attention(outer_body, "attention_outer", (held_pos, held, other, wqkv, wo, *early, coarse), W + HALF,
+    m0, m3 = attention(outer_body, "attention_outer", (held_pos, held, other, wqkv, wo, *early), W,
                        [], 5)
-    above = lax.ppermute(m3, "space", up)
-    below = lax.ppermute(m0, "space", down)
+    above, below = [lax.ppermute(m, "space", pairs) for m, pairs in zip((m0, m3), swaps)]
     wide = pltpu.VMEM((2, frames, C, W), F32)
-    m1, m2 = attention(inner_body, "attention_inner", (held_pos, held, other, wqkv, wo, m0), W,
+    m1, m2 = attention(inner_body, "attention_inner", (held_pos, held, other, wqkv, wo, coarse, m0), W + HALF,
                        [wide] * 3 + [pltpu.VMEM((2 * frames, C, W), BF16)], 7)
-    above2 = lax.ppermute(m2, "space", up)
-    below2 = lax.ppermute(m1, "space", down)
+    above2, below2 = [lax.ppermute(m, "space", pairs) for m, pairs in zip((m1, m2), swaps)]
     (mid,) = call(stage_one, "stage_one", (m0, m1, m2, m3, conv_first), [((frames, 2, W, C), BF16)],
                   [pads(4), planes(4)], 3)
     row = (frames, W, C)
@@ -358,10 +374,11 @@
         parts.append(call(functools.partial(stage_two, side), "stage_two_%d" % side,
                           (halo, near, far, mid, coarse, lift, conv_first, conv_second),
                           [(row, BF16), (row, F32), (row, F32)],
-                          [pads(6), planes(3), planes(3), pltpu.VMEM((2 * HALF, C), BF16)], 5))
+                          [pads(6), planes(3), planes(3)], 5))
     out = None
     for side, halo in enumerate((above2, below2)):
-        out = last_stage(side, "stage_three_%d" % side, (halo, *parts[side], conv_first, conv_second, parts[1 - side][0]),
+        out = last_stage(side, "stage_three_%d" % side, (halo, coarse, lift, *parts[side], conv_first, conv_second,
+                                                         parts[1 - side][0]),
                          out, fine.shape[1])
     return out
 

time: 50.9 us -> 50.2 us (0.986)
  the two profiles are of different devices: /device:TPU:30 before, /device:TPU:96 now
where the time goes in v4:
time: 50.2 us; the launch traced here: 50.1 us
  Pallas kernels  31.5 us (63%)
  starting transfers between devices  11.2 us (22%)
  waiting for transfers between devices  7 us (14%)
    pallas_call x6, Pallas kernels, call(): pl.pallas_call(body, in_specs=[pl.BlockSpec(memory_space=space)] * len(ar...  27.5 us
    ppermute x4, starting transfers between devices, local(): lax.ppermute(m, 'space', pairs)  11.2 us
    ppermute x4, waiting for transfers between devices, local(): lax.ppermute(m, 'space', pairs)  6.78 us
    pallas_call x2, Pallas kernels, last_stage(): pl.pallas_call(functools.partial(stage_three, side), in_specs=[pl.BlockSp...  4.02 us
  transfers between devices with their start and end apart: 5, of which 3 were waited for; matrix products, arithmetic and copies ran while one was open for 0% of the time, Pallas kernels for 52%

profile of v4, /device:TPU:96, one launch (start us, length us, event | category | flops | bytes accessed | tf_op | source)
XLA Modules:
  0.0 50.1 jit_solution(14641965558467976041)
XLA Ops:
  0.0 0.0 collective-permute-start
  0.0 4.1 %own_projections.1 = (f32[8,256,128]{2,1,0:T(8,128)S(1)}, bf16[4,4,256,256]{3,2,1,0:T(8,128)(2,1)S(1)}, bf16[768,256]{1,0:T(8,128)(2,1)S(1)}, bf16[256,256]{1,0:...) custom-call(f32[8,256,128]{2,1,0:T(8,128)} %constant.4.clone.pos_hbm, ...), custom_call_target="tpu_custom_call" | custom-call | flops 6000000000 | bytes 1048576 | tf_op jit(solution)/shard_map/own_projections/pallas_call | solution.py:190
  4.2 0.2 collective-permute-done.other_ref
  4.4 0.0 copy-start.2
  4.4 3.7 %attention_outer.1 = (bf16[4,256,256]{2,1,0:T(8,128)(2,1)S(1)}, bf16[4,256,256]{2,1,0:T(8,128)(2,1)S(1)}) custom-call(f32[8,256,128]{2,1,0:T(8,128)S(1)} %get-tuple-element.23.pos_ref, bf16[4,4,256,256]{3,2,1,0:T(8,128)(2,1)S(1)} %get-tuple-element.24.own_ref, bf16[4,4,256,256]{3,2,1,0:T(8,128)(2,1)S(1)} %collective-permute-done.other_ref, ...), custom_call_target="tpu_custom_call" | custom-call | flops 5000000000 | bytes 1048576 | tf_op jit(solution)/shard_map/attention_outer/pallas_call | solution.py:190
  8.1 7.0 %collective-permute-start.2 = (bf16[4,256,256]{2,1,0:T(8,128)(2,1)S(1)}, bf16[4,256,256]{2,1,0:T(8,128)(2,1)S(1)}, u32[]{:S(2)}, u32[]{:S(2)}) collective-permute-start(bf16[4,256,256]{2,1,0:T(8,128)(2,1)S(1)} %get-tuple-element.33.m3_ref.near_ref), channel_id=1, source_target_pairs={{1,2},{3,4},{5,6},{7,8},{9,10},{11,12},{13,14},{15,16},{17,18},{19... | collective-permute-start | bytes 1572872 | tf_op jit(solution)/shard_map/ppermute | solution.py:363
  15.1 0.0 copy-start
  15.1 0.1 collective-permute-start.3
  15.2 0.0 copy-done.2
  15.2 5.3 %attention_inner.1 = (bf16[4,384,256]{2,1,0:T(8,128)(2,1)S(1)}, bf16[4,384,256]{2,1,0:T(8,128)(2,1)S(1)}) custom-call(f32[8,256,128]{2,1,0:T(8,128)S(1)} %get-tuple-element.23.pos_ref, bf16[4,4,256,256]{3,2,1,0:T(8,128)(2,1)S(1)} %get-tuple-element.24.own_ref, bf16[4,4,256,256]{3,2,1,0:T(8,128)(2,1)S(1)} %collective-permute-done.other_ref, ...), custom_call_target="tpu_custom_call" | custom-call | flops 7000000000 | bytes 1048576 | tf_op jit(solution)/shard_map/attention_inner/pallas_call | solution.py:190
  20.5 3.2 %collective-permute-start.1 = (bf16[4,384,256]{2,1,0:T(8,128)(2,1)S(1)}, bf16[4,384,256]{2,1,0:T(8,128)(2,1)S(1)}, u32[]{:S(2)}, u32[]{:S(2)}) collective-permute-start(bf16[4,384,256]{2,1,0:T(8,128)(2,1)S(1)} %get-tuple-element.32.m2_ref.far_ref), channel_id=1, source_target_pairs={{1,2},{3,4},{5,6},{7,8},{9,10},{11,12},{13,14},{15,16},{17,18},{19... | collective-permute-start | bytes 2359304 | tf_op jit(solution)/shard_map/ppermute | solution.py:367
  23.7 0.0 copy-start.1
  23.7 0.0 copy-start.3
  23.8 0.9 %collective-permute-start.4 = (bf16[4,384,256]{2,1,0:T(8,128)(2,1)S(1)}, bf16[4,384,256]{2,1,0:T(8,128)(2,1)S(1)}, u32[]{:S(2)}, u32[]{:S(2)}) collective-permute-start(bf16[4,384,256]{2,1,0:T(8,128)(2,1)S(1)} %get-tuple-element.34.m1_ref.far_ref), channel_id=1, source_target_pairs={{0,1},{2,3},{4,5},{6,7},{8,9},{10,11},{12,13},{14,15},{16,17},{18,... | collective-permute-start | bytes 2359304 | tf_op jit(solution)/shard_map/ppermute | solution.py:367
  24.7 0.0 copy-done
  24.7 3.2 %stage_one.1.mid_ref = bf16[4,2,256,256]{3,2,1,0:T(8,128)(2,1)S(1)} custom-call(bf16[4,256,256]{2,1,0:T(8,128)(2,1)S(1)} %get-tuple-element.31.before_ref.m0_ref.near_ref, bf16[4,384,256]{2,1,0:T(8,128)(2,1)S(1)} %get-tuple-element.34.m1_ref.far_ref, bf16[4,384,256]{2,1,0:T(8,128)(2,1)S(1)} %get-tuple-element.32.m2_ref.far_ref, ...), custom_call_target="tpu_custom_call" | custom-call | flops 3000000000 | bytes 1048576 | tf_op jit(solution)/shard_map/stage_one/pallas_call | solution.py:190
  27.9 2.0 %collective-permute-done.3.halo_ref = bf16[4,256,256]{2,1,0:T(8,128)(2,1)S(1)} collective-permute-done((bf16[4,256,256]{2,1,0:T(8,128)(2,1)S(1)}, bf16[4,256,256]{2,1,0:T(8,128)(2,1)S(1)}, u32[]{:S(2)}, u32[]{:S(2)}) %collective-permute-start.3) | collective-permute-done | bytes 524320 | tf_op jit(solution)/shard_map/ppermute | solution.py:363
  29.9 0.0 copy-done.1
  29.9 0.0 copy-done.3
  30.0 6.2 %stage_two_0.1 = (bf16[4,256,256]{2,1,0:T(8,128)(2,1)S(1)}, f32[4,256,256]{2,1,0:T(8,128)S(1)}, f32[4,256,256]{2,1,0:T(8,128)S(1)}) custom-call(bf16[4,256,256]{2,1,0:T(8,128)(2,1)S(1)} %collective-permute-done.3.halo_ref, bf16[4,256,256]{2,1,0:T(8,128)(2,1)S(1)} %get-tuple-element.31.before_ref.m0_ref.near_ref, ...), custom_call_target="tpu_custom_call" | custom-call | flops 5000000000 | bytes 1048576 | tf_op jit(solution)/shard_map/stage_two_0/pallas_call | solution.py:190
  36.2 0.0 collective-permute-done.2.halo_ref
  36.2 4.9 %stage_two_1.1 = (bf16[4,256,256]{2,1,0:T(8,128)(2,1)S(1)}, f32[4,256,256]{2,1,0:T(8,128)S(1)}, f32[4,256,256]{2,1,0:T(8,128)S(1)}) custom-call(bf16[4,256,256]{2,1,0:T(8,128)(2,1)S(1)} %collective-permute-done.2.halo_ref, bf16[4,256,256]{2,1,0:T(8,128)(2,1)S(1)} %get-tuple-element.33.m3_ref.near_ref, ...), custom_call_target="tpu_custom_call" | custom-call | flops 5000000000 | bytes 1048576 | tf_op jit(solution)/shard_map/stage_two_1/pallas_call | solution.py:190
  41.1 4.7 %collective-permute-done.4.halo_ref = bf16[4,384,256]{2,1,0:T(8,128)(2,1)S(1)} collective-permute-done((bf16[4,384,256]{2,1,0:T(8,128)(2,1)S(1)}, bf16[4,384,256]{2,1,0:T(8,128)(2,1)S(1)}, u32[]{:S(2)}, u32[]{:S(2)}) %collective-permute-start.4) | collective-permute-done | bytes 786464 | tf_op jit(solution)/shard_map/ppermute | solution.py:367
  45.9 2.0 %stage_three_0.1.rest_1_ = bf16[4,4,256,256]{3,2,1,0:T(8,128)(2,1)} custom-call(bf16[4,384,256]{2,1,0:T(8,128)(2,1)S(1)} %collective-permute-done.4.halo_ref, bf16[4,2,128,256]{3,2,1,0:T(8,128)(2,1)S(1)} %copy-done.2, bf16[2,256,256]{2,1,0:T(8,128)(2,1)S(1)} %copy-done.3, bf16[4,256,256]{2,1,0:T(8,128)(2,1)S(1)} %get-tuple-element.38.inner_ref.rest_0_, ...), custom_call_target="tpu_custom_call" | custom-call | flops 2000000000 | bytes 1048576 | tf_op jit(solution)/shard_map/stage_three_0/pallas_call | solution.py:327
  47.9 0.0 collective-permute-done.1.halo_ref
  47.9 2.0 %stage_three_1.1 = bf16[4,4,256,256]{3,2,1,0:T(8,128)(2,1)} custom-call(bf16[4,384,256]{2,1,0:T(8,128)(2,1)S(1)} %collective-permute-done.1.halo_ref, bf16[4,2,128,256]{3,2,1,0:T(8,128)(2,1)S(1)} %copy-done.2, bf16[2,256,256]{2,1,0:T(8,128)(2,1)S(1)} %copy-done.3, ...), custom_call_target="tpu_custom_call", output_to_operand_aliasing={{}: (9, {})} | custom-call | flops 2000000000 | bytes 1048576 | tf_op jit(solution)/shard_map/stage_three_1/pallas_call | solution.py:327
Async XLA Ops:
  0.0 4.4 %collective-permute-start = (bf16[4,4,256,256]{3,2,1,0:T(8,128)(2,1)}, bf16[4,4,256,256]{3,2,1,0:T(8,128)(2,1)S(1)}, u32[]{:S(2)}, u32[]{:S(2)}) collective-permute-start(bf16[4,4,256,256]{3,2,1,0:T(8,128)(2,1)} %own_hbm.1), channel_id=1, source_target_pairs={{0,64},{64,0},{1,65},{65,1},{2,66},{66,2},{3,67},{67,3},{4,68},{68... | collective-permute-start | bytes 6291464 | tf_op jit(solution)/shard_map/ppermute | solution.py:357
  4.4 10.8 %copy-start.2 = (bf16[4,2,128,256]{3,2,1,0:T(8,128)(2,1)S(1)}, bf16[4,2,128,256]{3,2,1,0:T(8,128)(2,1)}, u32[]{:S(2)}) copy-start(bf16[4,2,128,256]{3,2,1,0:T(8,128)(2,1)} %coarse_ref.9) | copy-start | bytes 1572868
  8.1 28.1 %collective-permute-start.2 = (bf16[4,256,256]{2,1,0:T(8,128)(2,1)S(1)}, bf16[4,256,256]{2,1,0:T(8,128)(2,1)S(1)}, u32[]{:S(2)}, u32[]{:S(2)}) collective-permute-start(bf16[4,256,256]{2,1,0:T(8,128)(2,1)S(1)} %get-tuple-element.33.m3_ref.near_ref), channel_id=1, source_target_pairs={{1,2},{3,4},{5,6},{7,8},{9,10},{11,12},{13,14},{15,16},{17,18},{19... | collective-permute-start | bytes 1572872 | tf_op jit(solution)/shard_map/ppermute | solution.py:363
  15.1 9.6 %copy-start = (bf16[3,3,256,256]{3,2,1,0:T(8,128)(2,1)S(1)}, bf16[3,3,256,256]{3,2,1,0:T(8,128)(2,1)}, u32[]{:S(2)}) copy-start(bf16[3,3,256,256]{3,2,1,0:T(8,128)(2,1)} %w1_ref.9) | copy-start | bytes 3538948
  15.1 14.9 %collective-permute-start.3 = (bf16[4,256,256]{2,1,0:T(8,128)(2,1)S(1)}, bf16[4,256,256]{2,1,0:T(8,128)(2,1)S(1)}, u32[]{:S(2)}, u32[]{:S(2)}) collective-permute-start(bf16[4,256,256]{2,1,0:T(8,128)(2,1)S(1)} %get-tuple-element.31.before_ref.m0_ref.near_ref), channel_id=1, source_target_pairs={{0,1},{2,3},{4,5},{6,7},{8,9},{10,11},{12,13},{14,15},{16,17},{18,... | collective-permute-start | bytes 1572872 | tf_op jit(solution)/shard_map/ppermute | solution.py:363
  20.5 27.4 %collective-permute-start.1 = (bf16[4,384,256]{2,1,0:T(8,128)(2,1)S(1)}, bf16[4,384,256]{2,1,0:T(8,128)(2,1)S(1)}, u32[]{:S(2)}, u32[]{:S(2)}) collective-permute-start(bf16[4,384,256]{2,1,0:T(8,128)(2,1)S(1)} %get-tuple-element.32.m2_ref.far_ref), channel_id=1, source_target_pairs={{1,2},{3,4},{5,6},{7,8},{9,10},{11,12},{13,14},{15,16},{17,18},{19... | collective-permute-start | bytes 2359304 | tf_op jit(solution)/shard_map/ppermute | solution.py:367
  23.7 6.2 %copy-start.1 = (bf16[3,3,256,256]{3,2,1,0:T(8,128)(2,1)S(1)}, bf16[3,3,256,256]{3,2,1,0:T(8,128)(2,1)}, u32[]{:S(2)}) copy-start(bf16[3,3,256,256]{3,2,1,0:T(8,128)(2,1)} %w2_ref.7) | copy-start | bytes 3538948
  23.7 6.2 %copy-start.3 = (bf16[2,256,256]{2,1,0:T(8,128)(2,1)S(1)}, bf16[2,256,256]{2,1,0:T(8,128)(2,1)}, u32[]{:S(2)}) copy-start(bf16[2,256,256]{2,1,0:T(8,128)(2,1)} %constant.5.clone.lift_ref) | copy-start | bytes 786436
  23.8 22.1 %collective-permute-start.4 = (bf16[4,384,256]{2,1,0:T(8,128)(2,1)S(1)}, bf16[4,384,256]{2,1,0:T(8,128)(2,1)S(1)}, u32[]{:S(2)}, u32[]{:S(2)}) collective-permute-start(bf16[4,384,256]{2,1,0:T(8,128)(2,1)S(1)} %get-tuple-element.34.m1_ref.far_ref), channel_id=1, source_target_pairs={{0,1},{2,3},{4,5},{6,7},{8,9},{10,11},{12,13},{14,15},{16,17},{18,... | collective-permute-start | bytes 2359304 | tf_op jit(solution)/shard_map/ppermute | solution.py:367

commit v5 on v4

--- a/solution.py
+++ b/solution.py
@@ -7,6 +7,7 @@
 from jax.experimental import pallas as pl
 from jax.experimental.pallas import tpu as pltpu
 from jax.sharding import PartitionSpec as P
+
 
 HEADS = 8
 C = 256
@@ -132,7 +133,6 @@
 
 def own_body(pos_hbm, own_hbm, wq_hbm, wk_hbm, wv_hbm, wo_hbm,
              pos_ref, own_ref, wqkv_ref, wor_ref, q_ref, k_ref, v_ref, prior_ref, w_s, norm_s, sems):
-    frames, rows = own_hbm.shape[:2]
     loads = [pltpu.make_async_copy(ref, w_s.at[n], sems.at[n]) for n, ref in enumerate((wq_hbm, wk_hbm, wv_hbm, wo_hbm))]
     loads.append(pltpu.make_async_copy(pos_hbm, pos_ref, sems.at[4]))
     loads.append(pltpu.make_async_copy(own_hbm, own_ref, sems.at[5]))
@@ -186,7 +186,7 @@
         ref[:, W:] = coarse_ref[:, flip() ^ n]
 
 
-def call(body, name, args, outs, scratch, micros, space=pltpu.VMEM):
+def call(body, args, outs, scratch, micros, space=pltpu.VMEM):
     return pl.pallas_call(
         body,
         in_specs=[pl.BlockSpec(memory_space=space)] * len(args),
@@ -195,23 +195,22 @@
         scratch_shapes=scratch,
         compiler_params=pltpu.CompilerParams(vmem_limit_bytes=VMEM_LIMIT),
         cost_estimate=pl.CostEstimate(flops=micros * 10**9, transcendentals=0, bytes_accessed=1 << 20),
-        name=name,
     )(*args)
 
 
 def own_projections(pos, own, *weights):
-    frames, rows = own.shape[:2]
+    frames, _ = own.shape[:2]
     wide = ((2, frames, C, W), F32)
     args = [pltpu.with_memory_space_constraint(a, pltpu.HBM) for a in (pos, own, *weights)]
-    return call(own_body, "own_projections", args,
+    return call(own_body, args,
                 [(pos.shape, F32), (own.shape, BF16), ((3 * C, C), BF16), ((C, C), BF16), wide, wide, wide,
                  ((2, W // 128, frames * frames, HEADS, 128), F32)],
                 [pltpu.VMEM((4, C, C), BF16), pltpu.VMEM((2 * frames, C, W), BF16), pltpu.SemaphoreType.DMA((6,))], 6, pltpu.HBM)
 
 
-def attention(body, name, args, width, extra, micros):
+def attention(body, args, width, extra, micros):
     frames = args[1].shape[0]
-    return call(body, name, args, [((frames, width, C), BF16)] * 2,
+    return call(body, args, [((frames, width, C), BF16)] * 2,
                 [pltpu.VMEM((2 * frames, C, W), BF16), pltpu.VMEM((2, frames, C, W), F32),
                  pltpu.VMEM((2, frames, C, W), F32), pltpu.VMEM((2, frames, C, W), BF16)] + extra, micros)
 
@@ -295,48 +294,52 @@
     lax.fori_loop(0, near_ref.shape[0], frame, 0)
 
 
-def stage_three(side, halo_ref, coarse_ref, lift_ref, inner_ref, first_ref, second_ref, w1_ref, w2_ref, *rest):
-    out_hbm, pad_s, in_s, mid_s, row_s, coarse_s, sems = rest[-7:]
-    edge = at_edge(side)
-    near = flip() ^ side
-    frames = halo_ref.shape[0]
-    copies = [pltpu.make_async_copy(inner_ref.at[f], out_hbm.at[f, 1 + near], sems.at[f]) for f in range(frames)]
-    copies += [pltpu.make_async_copy(row_s.at[f], out_hbm.at[f, 3 * near], sems.at[frames + f]) for f in range(frames)]
-    for copy in copies[:frames]:
-        copy.start()
+def stage_three(*refs):
+    halos, coarse_ref, lift_ref, parts, w1_ref, w2_ref = refs[:2], refs[2], refs[3], (refs[4:7], refs[7:10]), refs[10], refs[11]
+    out_hbm, pad_s, in_s, mid_s, row_s, coarse_s, sems = refs[12:]
+    frames = halos[0].shape[0]
+    copies = []
+    for side in range(2):
+        for f in range(frames):
+            n = side * frames + f
+            copies.append(pltpu.make_async_copy(parts[side][0].at[f], out_hbm.at[f, 1 + (flip() ^ side)], sems.at[n]))
+            copies[-1].start()
     clear_pads(pad_s)
-    step = (2 * side,)
-    for f in range(frames):
-        shifted(relu(halo_ref[f, :W]), pad_s.at[f], in_s, f)
-        own = coarse_ref[f, near]
-        coarse_s[f, :HALF] = jnp.where(edge, own, halo_ref[f, W:])
-        coarse_s[f, HALF:] = own
-        value = relu(taps(in_s, f, w1_ref, first_ref[f], step)).astype(BF16)
-        value = jnp.where(edge, jnp.zeros_like(value), value)
-        shifted(value, pad_s.at[frames + f], mid_s, f)
-        total = second_ref[f] + dot(lift_ref[0], coarse_s[f])
-        row_s[f] = taps(mid_s, f, w2_ref, total, step).astype(BF16)
-        copies[frames + f].start()
+    for side in range(2):
+        edge = at_edge(side)
+        near = flip() ^ side
+        step = (2 * side,)
+        for f in range(frames):
+            n = side * frames + f
+            halo_ref, first_ref, second_ref = halos[side], parts[side][1], parts[side][2]
+            shifted(relu(halo_ref[f, :W]), pad_s.at[n], in_s, n)
+            own = coarse_ref[f, near]
+            coarse_s[n, :HALF] = jnp.where(edge, own, halo_ref[f, W:])
+            coarse_s[n, HALF:] = own
+            value = relu(taps(in_s, n, w1_ref, first_ref[f], step)).astype(BF16)
+            value = jnp.where(edge, jnp.zeros_like(value), value)
+            shifted(value, pad_s.at[2 * frames + n], mid_s, n)
+            total = second_ref[f] + dot(lift_ref[0], coarse_s[n])
+            row_s[n] = taps(mid_s, n, w2_ref, total, step).astype(BF16)
+            copies.append(pltpu.make_async_copy(row_s.at[n], out_hbm.at[f, 3 * near], sems.at[2 * frames + n]))
+            copies[-1].start()
     for copy in copies:
         copy.wait()
 
 
-def last_stage(side, name, args, out, rows):
+def last_stage(args, rows):
     frames = args[0].shape[0]
-    before = [] if out is None else [out]
     return pl.pallas_call(
-        functools.partial(stage_three, side),
-        in_specs=[pl.BlockSpec(memory_space=pltpu.VMEM)] * len(args)
-        + [pl.BlockSpec(memory_space=pltpu.HBM)] * len(before),
+        stage_three,
+        in_specs=[pl.BlockSpec(memory_space=pltpu.VMEM)] * len(args),
         out_specs=pl.BlockSpec(memory_space=pltpu.HBM),
         out_shape=jax.ShapeDtypeStruct((frames, rows, W, C), BF16),
-        scratch_shapes=[pads(2 * frames), planes(frames), planes(frames), pltpu.VMEM((frames, W, C), BF16),
-                        pltpu.VMEM((frames, 2 * HALF, C), BF16), pltpu.SemaphoreType.DMA((2 * frames,))],
-        input_output_aliases={len(args): 0} if before else {},
+        scratch_shapes=[pads(4 * frames), planes(2 * frames), planes(2 * frames), pltpu.VMEM((2 * frames, W, C), BF16),
+                        pltpu.VMEM((2 * frames, 2 * HALF, C), BF16), pltpu.SemaphoreType.DMA((4 * frames,))],
         compiler_params=pltpu.CompilerParams(vmem_limit_bytes=VMEM_LIMIT),
-        cost_estimate=pl.CostEstimate(flops=2 * 10**9, transcendentals=0, bytes_accessed=1 << 20),
-        name=name,
-    )(*args, *before)
+        cost_estimate=pl.CostEstimate(flops=4 * 10**9, transcendentals=0, bytes_accessed=1 << 20),
+        name="stage_three",
+    )(*args)
 
 
 def planes(rows):
@@ -358,28 +361,25 @@
     pos = jnp.asarray(encode_table(2 * frames, C))
     ready = own_projections(pos, fine, w_query, w_key, w_value, w_out)
     held_pos, held, wqkv, wo, *early = ready
-    m0, m3 = attention(outer_body, "attention_outer", (held_pos, held, other, wqkv, wo, *early), W,
+    m0, m3 = attention(outer_body, (held_pos, held, other, wqkv, wo, *early), W,
                        [], 5)
     above, below = [lax.ppermute(m, "space", pairs) for m, pairs in zip((m0, m3), swaps)]
     wide = pltpu.VMEM((2, frames, C, W), F32)
-    m1, m2 = attention(inner_body, "attention_inner", (held_pos, held, other, wqkv, wo, coarse, m0), W + HALF,
+    m1, m2 = attention(inner_body, (held_pos, held, other, wqkv, wo, coarse, m0), W + HALF,
                        [wide] * 3 + [pltpu.VMEM((2 * frames, C, W), BF16)], 7)
-    above2, below2 = [lax.ppermute(m, "space", pairs) for m, pairs in zip((m1, m2), swaps)]
-    (mid,) = call(stage_one, "stage_one", (m0, m1, m2, m3, conv_first), [((frames, 2, W, C), BF16)],
+    above2 = lax.ppermute(m1, "space", swaps[0])
+    below2 = lax.ppermute(m2, "space", swaps[1])
+    (mid,) = call(stage_one, (m0, m1, m2, m3, conv_first), [((frames, 2, W, C), BF16)],
                   [pads(4), planes(4)], 3)
     row = (frames, W, C)
     lift = jnp.asarray(lift_matrices(), BF16)
     parts = []
     for side, (halo, near, far) in enumerate(((above, m0, m1), (below, m3, m2))):
-        parts.append(call(functools.partial(stage_two, side), "stage_two_%d" % side,
+        parts.append(call(functools.partial(stage_two, side),
                           (halo, near, far, mid, coarse, lift, conv_first, conv_second),
                           [(row, BF16), (row, F32), (row, F32)],
                           [pads(6), planes(3), planes(3)], 5))
-    out = None
-    for side, halo in enumerate((above2, below2)):
-        out = last_stage(side, "stage_three_%d" % side, (halo, coarse, lift, *parts[side], conv_first, conv_second,
-                                                         parts[1 - side][0]),
-                         out, fine.shape[1])
+    out = last_stage((above2, below2, coarse, lift, *parts[0], *parts[1], conv_first, conv_second), fine.shape[1])
     return out
 
 

time: 50.2 us -> 51.2 us (1.020)
  starting transfers between devices: 11.2 us -> 12.5 us
  Pallas kernels: 31.5 us -> 30.7 us
  waiting for transfers between devices: 7 us -> 7.53 us
    ppermute x0 -> x2, waiting for transfers between devices: none -> 7.3 us  [the longest x1 5.44 us: local(): above2 = lax.ppermute(m1, 'space', swaps[0])]
    ppermute x4 -> x2, waiting for transfers between devices: 6.78 us -> 0.01 us  [local(): lax.ppermute(m, 'space', pairs)]
    ppermute x0 -> x2, starting transfers between devices: none -> 5.48 us  [the longest x1 3.41 us: local(): below2 = lax.ppermute(m2, 'space', swaps[1])]
    ppermute x4 -> x2, starting transfers between devices: 11.2 us -> 7.04 us  [local(): lax.ppermute(m, 'space', pairs)]
    pallas_call x2 -> x1, Pallas kernels: 4.02 us -> 3.2 us  [last_stage(): pl.pallas_call(stage_three, in_specs=[pl.BlockSpec(memory_space=pltpu.VME...]
  transfers between devices with their start and end apart: 5 -> 5, of which waited for: 3 -> 3; matrix products, arithmetic and copies ran while one was open for 0% -> 0% of each run, Pallas kernels for 52% -> 47%
where the time goes in v5:
time: 51.2 us; the launch traced here: 51.1 us
  Pallas kernels  30.7 us (60%)
  starting transfers between devices  12.5 us (24%)
  waiting for transfers between devices  7.53 us (15%)
    pallas_call x6, Pallas kernels, call(): pl.pallas_call(body, in_specs=[pl.BlockSpec(memory_space=space)] * len(ar...  27.5 us
    ppermute x2, starting transfers between devices, local(): lax.ppermute(m, 'space', pairs)  7.04 us
    ppermute x1, waiting for transfers between devices, local(): above2 = lax.ppermute(m1, 'space', swaps[0])  5.44 us
    ppermute x1, starting transfers between devices, local(): below2 = lax.ppermute(m2, 'space', swaps[1])  3.41 us
    pallas_call x1, Pallas kernels, last_stage(): pl.pallas_call(stage_three, in_specs=[pl.BlockSpec(memory_space=pltpu.VME...  3.2 us
    ppermute x1, starting transfers between devices, local(): above2 = lax.ppermute(m1, 'space', swaps[0])  2.07 us
    ppermute x1, waiting for transfers between devices, local(): below2 = lax.ppermute(m2, 'space', swaps[1])  1.86 us
  transfers between devices with their start and end apart: 5, of which 3 were waited for; matrix products, arithmetic and copies ran while one was open for 0% of the time, Pallas kernels for 47%

profile of v5, /device:TPU:96, one launch (start us, length us, event | category | flops | bytes accessed | tf_op | source)
XLA Modules:
  0.0 51.1 jit_solution(14995554020872811497)
XLA Ops:
  0.0 0.0 collective-permute-start
  0.0 4.1 %shard_map.100 = (f32[8,256,128]{2,1,0:T(8,128)S(1)}, bf16[4,4,256,256]{3,2,1,0:T(8,128)(2,1)S(1)}, bf16[768,256]{1,0:T(8,128)(2,1)S(1)}, bf16[256,256]{1,0:T(8,...) custom-call(f32[8,256,128]{2,1,0:T(8,128)} %constant.4.clone.pos_hbm, ...), custom_call_target="tpu_custom_call" | custom-call | flops 6000000000 | bytes 1048576 | tf_op jit(solution)/shard_map/pallas_call | solution.py:190
  4.2 0.2 collective-permute-done.other_ref
  4.4 0.0 copy-start.2
  4.4 3.7 %shard_map.101 = (bf16[4,256,256]{2,1,0:T(8,128)(2,1)S(1)}, bf16[4,256,256]{2,1,0:T(8,128)(2,1)S(1)}) custom-call(f32[8,256,128]{2,1,0:T(8,128)S(1)} %get-tuple-element.23.pos_ref, bf16[4,4,256,256]{3,2,1,0:T(8,128)(2,1)S(1)} %get-tuple-element.24.own_ref, bf16[4,4,256,256]{3,2,1,0:T(8,128)(2,1)S(1)} %collective-permute-done.other_ref, ...), custom_call_target="tpu_custom_call" | custom-call | flops 5000000000 | bytes 1048576 | tf_op jit(solution)/shard_map/pallas_call | solution.py:190
  8.1 7.0 %collective-permute-start.4 = (bf16[4,256,256]{2,1,0:T(8,128)(2,1)S(1)}, bf16[4,256,256]{2,1,0:T(8,128)(2,1)S(1)}, u32[]{:S(2)}, u32[]{:S(2)}) collective-permute-start(bf16[4,256,256]{2,1,0:T(8,128)(2,1)S(1)} %get-tuple-element.34.m3_ref.near_ref), channel_id=1, source_target_pairs={{1,2},{3,4},{5,6},{7,8},{9,10},{11,12},{13,14},{15,16},{17,18},{19... | collective-permute-start | bytes 1572872 | tf_op jit(solution)/shard_map/ppermute | solution.py:366
  15.1 0.0 copy-start
  15.1 0.1 collective-permute-start.3
  15.2 0.0 copy-done.2
  15.2 5.3 %shard_map.102 = (bf16[4,384,256]{2,1,0:T(8,128)(2,1)S(1)}, bf16[4,384,256]{2,1,0:T(8,128)(2,1)S(1)}) custom-call(f32[8,256,128]{2,1,0:T(8,128)S(1)} %get-tuple-element.23.pos_ref, bf16[4,4,256,256]{3,2,1,0:T(8,128)(2,1)S(1)} %get-tuple-element.24.own_ref, bf16[4,4,256,256]{3,2,1,0:T(8,128)(2,1)S(1)} %collective-permute-done.other_ref, ...), custom_call_target="tpu_custom_call" | custom-call | flops 7000000000 | bytes 1048576 | tf_op jit(solution)/shard_map/pallas_call | solution.py:190
  20.5 2.1 %collective-permute-start.1 = (bf16[4,384,256]{2,1,0:T(8,128)(2,1)S(1)}, bf16[4,384,256]{2,1,0:T(8,128)(2,1)S(1)}, u32[]{:S(2)}, u32[]{:S(2)}) collective-permute-start(bf16[4,384,256]{2,1,0:T(8,128)(2,1)S(1)} %get-tuple-element.32.m1_ref.far_ref), channel_id=1, source_target_pairs={{0,1},{2,3},{4,5},{6,7},{8,9},{10,11},{12,13},{14,15},{16,17},{18,... | collective-permute-start | bytes 2359304 | tf_op jit(solution)/shard_map/ppermute | solution.py:370
  22.6 0.0 copy-start.1
  22.6 0.0 copy-start.3
  22.6 3.4 %collective-permute-start.2 = (bf16[4,384,256]{2,1,0:T(8,128)(2,1)S(1)}, bf16[4,384,256]{2,1,0:T(8,128)(2,1)S(1)}, u32[]{:S(2)}, u32[]{:S(2)}) collective-permute-start(bf16[4,384,256]{2,1,0:T(8,128)(2,1)S(1)} %get-tuple-element.33.m2_ref.far_ref), channel_id=1, source_target_pairs={{1,2},{3,4},{5,6},{7,8},{9,10},{11,12},{13,14},{15,16},{17,18},{19... | collective-permute-start | bytes 2359304 | tf_op jit(solution)/shard_map/ppermute | solution.py:371
  26.0 0.0 copy-done
  26.0 3.2 %shard_map.103.mid_ref = bf16[4,2,256,256]{3,2,1,0:T(8,128)(2,1)S(1)} custom-call(bf16[4,256,256]{2,1,0:T(8,128)(2,1)S(1)} %get-tuple-element.31.before_ref.m0_ref.near_ref, bf16[4,384,256]{2,1,0:T(8,128)(2,1)S(1)} %get-tuple-element.32.m1_ref.far_ref, bf16[4,384,256]{2,1,0:T(8,128)(2,1)S(1)} %get-tuple-element.33.m2_ref.far_ref, ...), custom_call_target="tpu_custom_call" | custom-call | flops 3000000000 | bytes 1048576 | tf_op jit(solution)/shard_map/pallas_call | solution.py:190
  29.2 0.0 collective-permute-done.4.halo_ref
  29.2 0.0 copy-done.1
  29.2 0.0 copy-done.3
  29.2 4.9 %shard_map.105 = (bf16[4,256,256]{2,1,0:T(8,128)(2,1)S(1)}, f32[4,256,256]{2,1,0:T(8,128)S(1)}, f32[4,256,256]{2,1,0:T(8,128)S(1)}) custom-call(bf16[4,256,256]{2,1,0:T(8,128)(2,1)S(1)} %collective-permute-done.4.halo_ref, bf16[4,256,256]{2,1,0:T(8,128)(2,1)S(1)} %get-tuple-element.34.m3_ref.near_ref, ...), custom_call_target="tpu_custom_call" | custom-call | flops 5000000000 | bytes 1048576 | tf_op jit(solution)/shard_map/pallas_call | solution.py:190
  34.2 0.0 collective-permute-done.3.halo_ref
  34.2 6.2 %shard_map.104 = (bf16[4,256,256]{2,1,0:T(8,128)(2,1)S(1)}, f32[4,256,256]{2,1,0:T(8,128)S(1)}, f32[4,256,256]{2,1,0:T(8,128)S(1)}) custom-call(bf16[4,256,256]{2,1,0:T(8,128)(2,1)S(1)} %collective-permute-done.3.halo_ref, bf16[4,256,256]{2,1,0:T(8,128)(2,1)S(1)} %get-tuple-element.31.before_ref.m0_ref.near_ref, ...), custom_call_target="tpu_custom_call" | custom-call | flops 5000000000 | bytes 1048576 | tf_op jit(solution)/shard_map/pallas_call | solution.py:190
  40.4 5.4 %collective-permute-done.1.refs_0_ = bf16[4,384,256]{2,1,0:T(8,128)(2,1)S(1)} collective-permute-done((bf16[4,384,256]{2,1,0:T(8,128)(2,1)S(1)}, bf16[4,384,256]{2,1,0:T(8,128)(2,1)S(1)}, u32[]{:S(2)}, u32[]{:S(2)}) %collective-permute-start.1) | collective-permute-done | bytes 786464 | tf_op jit(solution)/shard_map/ppermute | solution.py:370
  45.9 1.9 %collective-permute-done.2.refs_1_ = bf16[4,384,256]{2,1,0:T(8,128)(2,1)S(1)} collective-permute-done((bf16[4,384,256]{2,1,0:T(8,128)(2,1)S(1)}, bf16[4,384,256]{2,1,0:T(8,128)(2,1)S(1)}, u32[]{:S(2)}, u32[]{:S(2)}) %collective-permute-start.2) | collective-permute-done | bytes 786464 | tf_op jit(solution)/shard_map/ppermute | solution.py:371
  47.7 3.2 %stage_three.1 = bf16[4,4,256,256]{3,2,1,0:T(8,128)(2,1)} custom-call(bf16[4,384,256]{2,1,0:T(8,128)(2,1)S(1)} %collective-permute-done.1.refs_0_, bf16[4,384,256]{2,1,0:T(8,128)(2,1)S(1)} %collective-permute-done.2.refs_1_, bf16[4,2,128,256]{3,2,1,0:T(8,128)(2,1)S(1)} %copy-done.2, bf16[2,256,256]{2,1,0:T(8,128)(2,1)S(1)} %copy-done.3, ...), custom_call_target="tpu_custom_call" | custom-call | flops 4000000000 | bytes 1048576 | tf_op jit(solution)/shard_map/stage_three/pallas_call | solution.py:332
Async XLA Ops:
  0.0 4.4 %collective-permute-start = (bf16[4,4,256,256]{3,2,1,0:T(8,128)(2,1)}, bf16[4,4,256,256]{3,2,1,0:T(8,128)(2,1)S(1)}, u32[]{:S(2)}, u32[]{:S(2)}) collective-permute-start(bf16[4,4,256,256]{3,2,1,0:T(8,128)(2,1)} %own_hbm.1), channel_id=1, source_target_pairs={{0,64},{64,0},{1,65},{65,1},{2,66},{66,2},{3,67},{67,3},{4,68},{68... | collective-permute-start | bytes 6291464 | tf_op jit(solution)/shard_map/ppermute | solution.py:360
  4.4 10.8 %copy-start.2 = (bf16[4,2,128,256]{3,2,1,0:T(8,128)(2,1)S(1)}, bf16[4,2,128,256]{3,2,1,0:T(8,128)(2,1)}, u32[]{:S(2)}) copy-start(bf16[4,2,128,256]{3,2,1,0:T(8,128)(2,1)} %refs_2_.1) | copy-start | bytes 1572868
  8.1 21.1 %collective-permute-start.4 = (bf16[4,256,256]{2,1,0:T(8,128)(2,1)S(1)}, bf16[4,256,256]{2,1,0:T(8,128)(2,1)S(1)}, u32[]{:S(2)}, u32[]{:S(2)}) collective-permute-start(bf16[4,256,256]{2,1,0:T(8,128)(2,1)S(1)} %get-tuple-element.34.m3_ref.near_ref), channel_id=1, source_target_pairs={{1,2},{3,4},{5,6},{7,8},{9,10},{11,12},{13,14},{15,16},{17,18},{19... | collective-permute-start | bytes 1572872 | tf_op jit(solution)/shard_map/ppermute | solution.py:366
  15.1 10.9 %copy-start = (bf16[3,3,256,256]{3,2,1,0:T(8,128)(2,1)S(1)}, bf16[3,3,256,256]{3,2,1,0:T(8,128)(2,1)}, u32[]{:S(2)}) copy-start(bf16[3,3,256,256]{3,2,1,0:T(8,128)(2,1)} %refs_10_.1) | copy-start | bytes 3538948
  15.1 19.1 %collective-permute-start.3 = (bf16[4,256,256]{2,1,0:T(8,128)(2,1)S(1)}, bf16[4,256,256]{2,1,0:T(8,128)(2,1)S(1)}, u32[]{:S(2)}, u32[]{:S(2)}) collective-permute-start(bf16[4,256,256]{2,1,0:T(8,128)(2,1)S(1)} %get-tuple-element.31.before_ref.m0_ref.near_ref), channel_id=1, source_target_pairs={{0,1},{2,3},{4,5},{6,7},{8,9},{10,11},{12,13},{14,15},{16,17},{18,... | collective-permute-start | bytes 1572872 | tf_op jit(solution)/shard_map/ppermute | solution.py:366
  20.5 25.4 %collective-permute-start.1 = (bf16[4,384,256]{2,1,0:T(8,128)(2,1)S(1)}, bf16[4,384,256]{2,1,0:T(8,128)(2,1)S(1)}, u32[]{:S(2)}, u32[]{:S(2)}) collective-permute-start(bf16[4,384,256]{2,1,0:T(8,128)(2,1)S(1)} %get-tuple-element.32.m1_ref.far_ref), channel_id=1, source_target_pairs={{0,1},{2,3},{4,5},{6,7},{8,9},{10,11},{12,13},{14,15},{16,17},{18,... | collective-permute-start | bytes 2359304 | tf_op jit(solution)/shard_map/ppermute | solution.py:370
  22.6 6.6 %copy-start.1 = (bf16[3,3,256,256]{3,2,1,0:T(8,128)(2,1)S(1)}, bf16[3,3,256,256]{3,2,1,0:T(8,128)(2,1)}, u32[]{:S(2)}) copy-start(bf16[3,3,256,256]{3,2,1,0:T(8,128)(2,1)} %refs_11_.1) | copy-start | bytes 3538948
  22.6 6.6 %copy-start.3 = (bf16[2,256,256]{2,1,0:T(8,128)(2,1)S(1)}, bf16[2,256,256]{2,1,0:T(8,128)(2,1)}, u32[]{:S(2)}) copy-start(bf16[2,256,256]{2,1,0:T(8,128)(2,1)} %constant.5.clone.lift_ref.refs_3_) | copy-start | bytes 786436
  22.6 25.2 %collective-permute-start.2 = (bf16[4,384,256]{2,1,0:T(8,128)(2,1)S(1)}, bf16[4,384,256]{2,1,0:T(8,128)(2,1)S(1)}, u32[]{:S(2)}, u32[]{:S(2)}) collective-permute-start(bf16[4,384,256]{2,1,0:T(8,128)(2,1)S(1)} %get-tuple-element.33.m2_ref.far_ref), channel_id=1, source_target_pairs={{1,2},{3,4},{5,6},{7,8},{9,10},{11,12},{13,14},{15,16},{17,18},{19... | collective-permute-start | bytes 2359304 | tf_op jit(solution)/shard_map/ppermute | solution.py:371
